TPU v7x, 256 devices: a whole 4x4x8 slice. The times are simulated.
256 devices in a mesh: node: 128 (over x_lo, z, y, core), blk: 2 (over x_hi).
Axes of the slice: x: 4 (x_hi: 2, x_lo: 2; x = x_hi * 2 + x_lo), y: 4, z: 8, core: 2. Of those that a mesh axis runs over, the one named last changes fastest.
Arguments:
- params: bfloat16 [128, 128, 14336], P('node', 'blk'), may hold values from -40 to 40
- weights: int32 [128], P('node'), may hold values from 1 to 8
Outputs:
- debiased: float32 [128, 128, 14336], P('node', 'blk')
- average: float32 [128, 14336], P('blk', 'node')
- spread: float32 [128], P('node')
All inputs are finite; a program needn't handle non-finite values.
Results may differ from a plain program's by a relative error of at most 0.0003.
Values may be sent and summed in bfloat16 or wider, within the bound.
No kernel may reach another device: no remote copies, remote signals or barrier semaphores. Data moves between devices by JAX's collectives and lax.ppermute only.
A program may use at most 64 MiB of HBM per device.

v0:
```python
import jax
import jax.numpy as jnp
from jax import lax
from jax.sharding import Mesh
from jax.sharding import PartitionSpec as P

ROUNDS = 3
NODE = ("node_0", "node_1", "node_2", "node_3")


def from_behind(value, axis, steps):
    count = lax.axis_size(axis)
    pairs = [(source, (source + steps) % count) for source in range(count)]
    return lax.ppermute(value, axis, pairs)


def cut_along(value, dim, size):
    lengths = value.shape
    pieces = value.reshape(*lengths[:dim], size, lengths[dim] // size, *lengths[dim + 1 :])
    return jnp.moveaxis(pieces, dim, 0)


def sent_and_summed(value, axis, dim):
    size = lax.axis_size(axis)
    pieces = lax.all_to_all(cut_along(value, dim, size), axis, 0, 0, tiled=True)
    return jnp.sum(pieces, axis=0)


def sum_by_axis(value, axes, dim):
    far, near = axes
    own = sent_and_summed(cut_along(value, dim, lax.axis_size(far)), near, dim + 1)
    return jnp.sum(lax.all_to_all(own, far, 0, 0, tiled=True), axis=0)


def padded_to(lines, size):
    spare = -lines.shape[0] % size
    if not spare:
        return lines
    return jnp.concatenate([lines, jnp.zeros((spare, *lines.shape[1:]), lines.dtype)])


def sent_to_all(value, axis):
    size = lax.axis_size(axis)
    return lax.all_to_all(
        jnp.broadcast_to(value[None], (size, *value.shape)), axis, 0, 0, tiled=True
    )


def in_order(pieces, dim):
    pieces = jnp.moveaxis(pieces, 0, dim)
    lengths = pieces.shape
    return pieces.reshape(*lengths[:dim], lengths[dim] * lengths[dim + 1], *lengths[dim + 2 :])


def whole_of(value, axes, dim):
    far, near = axes
    pieces = sent_to_all(sent_to_all(value, far), near)
    return in_order(pieces.swapaxes(0, 1).reshape(-1, *value.shape), dim)


def sum_by_parts(value, axes):
    own = sum_by_axis(padded_to(value, lax.axis_size(axes[0]) * lax.axis_size(axes[1])), axes, 0)
    whole = whole_of(own, axes, 0)
    return whole[: len(value)].reshape(value.shape)


def packed_total(arrays, axis):
    ravelled, at, done = (jnp.concatenate([a.reshape(-1) for a in arrays]), 0, [])
    total = sum_by_parts(ravelled, axis)
    for a in arrays:
        done.append(total[at : at + a.size].reshape(a.shape))
        at += a.size
    return tuple(done)


def of_everyone(value, axis):
    everything = sent_to_all(value, axis)
    return jnp.sum(everything, axis=0)


def push_round(value, scale, hop):
    received = from_behind((value, scale), NODE, hop)
    return (received[0], received[1])


def shards(params, weights):
    node_count = lax.axis_size(NODE)
    levels = node_count.bit_length() - 1
    scale0 = weights.astype(jnp.float32)
    weighted = scale0[:, None, None] * params.astype(jnp.float32)
    value = weighted
    scale = scale0
    for step in range(ROUNDS):
        hop = 1 << step % levels
        other_value, other_scale = push_round(value, scale, hop)
        value = 0.5 * value + 0.5 * other_value
        scale = 0.5 * scale + 0.5 * other_scale
    debiased = value / scale[:, None, None]
    hidden_units = params.shape[2]
    width = hidden_units // node_count
    local = debiased[0]
    numer, total = packed_total(
        (weighted[0], jnp.sum(scale0)), (("node_0", "node_1", "node_2"), "node_3")
    )
    whole = numer / total
    partial_value = jnp.sum((local - whole) ** 2)[None]
    average = lax.dynamic_slice_in_dim(whole, lax.axis_index(NODE) * width, width, 1)
    row_count = params.shape[1] * lax.axis_size("blk")
    spread = of_everyone(partial_value, "blk") / (row_count * hidden_units)
    return (debiased, average, spread)


def solution(mesh):
    finer = Mesh(
        mesh.devices.reshape(2, 8, 4, 2, mesh.shape["blk"]),
        ("node_0", "node_1", "node_2", "node_3", "blk"),
    )
    return jax.shard_map(
        shards,
        mesh=finer,
        in_specs=(P(NODE, "blk", None), P(NODE)),
        out_specs=(P(NODE, "blk", None), P("blk", NODE), P(NODE)),
        check_vma=False,
    )
```

profile of v0, /device:TPU:2, one launch (start us, length us, event | category | flops | bytes accessed | tf_op | source)
XLA Modules:
  0.0 408.1 jit_solution(10509269107073951939)
XLA Ops:
  1.4 1.7 convert_multiply_fusion
  3.3 48.3 %collective-permute-done = f32[1,64,14336]{2,1,0:T(8,128)S(1)} collective-permute-done((f32[1,64,14336]{2,1,0:T(8,128)S(1)}, f32[1,64,14336]{2,1,0:T(8,128)S(1)}, u32[]{:S(2)}, u32[]{:S(2)}) %collective-permute-start) | collective-permute-done | bytes 3670048 | tf_op jit(solution)/shard_map/ppermute | solution.py:14
  52.1 79.1 %collective-permute-done.1 = f32[1,64,14336]{2,1,0:T(8,128)S(1)} collective-permute-done((f32[1,64,14336]{2,1,0:T(8,128)S(1)}, f32[1,64,14336]{2,1,0:T(8,128)S(1)}, u32[]{:S(2)}, u32[]{:S(2)}) %collective-permute-start.1) | collective-permute-done | bytes 3670048 | tf_op jit(solution)/shard_map/ppermute | solution.py:14
  131.3 2.7 multiply_add_fusion
  134.0 2.5 copy.15
  136.4 29.5 %concatenate.3 = f32[917632]{0:T(1024)} concatenate(f32[917504]{0:T(1024)} %bitcast.20, f32[1]{0:T(128)} %convert_element_type.6, f32[127]{0:T(128)S(1)} %broadcast_in_dim.10), dimensions={0} | concatenate | bytes 7341056 | tf_op jit(solution)/shard_map/concatenate | solution.py:39
  165.9 7.6 %reshape_reshape.6 = f32[64,2,7169]{2,1,0:T(2,128)} reshape(f32[917632]{0:T(1024)} %concatenate.3) | data formatting | bytes 7341056 | tf_op jit(solution)/shard_map/reshape;reshape | solution.py:19
  173.5 2.3 copy.10
  175.8 7.8 %all_to_all.31 = f32[2,64,7169]{2,1,0:T(8,128)} all-to-all(f32[2,64,7169]{2,1,0:T(8,128)S(1)} %copy.10), channel_id=1, replica_groups=mesh['node_0'=2,'node_1'=8,'node_2'=4,'node_3'=2,'blk'=2] {'node_3'}, dimensions={0} | all-to-all | bytes 7341056 | tf_op jit(solution)/shard_map/all_to_all | solution.py:25
  183.6 2.5 reduce_sum.40
  186.1 1.3 all_to_all.21
  187.4 53.7 %all_to_all.32 = f32[64,1,7169]{2,1,0:T(1,128)S(1)} all-to-all(f32[64,1,7169]{2,1,0:T(1,128)S(1)} %all_to_all.21), channel_id=1, replica_groups=mesh['node_0'=2,'node_1'=8,'node_2'=4,'node_3'=2,'blk'=2] {'node_0','nod..., dimensions={0} | all-to-all | bytes 3670528 | tf_op jit(solution)/shard_map/all_to_all | solution.py:32
  241.1 1.1 reduce_sum.41
  242.2 2.2 broadcast_in_dim.11
  244.4 7.8 %all-to-all-start.2 = ((f32[64,1,7169]{2,1,0:T(1,128)}), f32[64,1,7169]{2,1,0:T(1,128)S(1)}, u32[]{:S(2)}, u32[]{:S(2)}) async-start(f32[64,1,7169]{2,1,0:T(1,128)} %broadcast_in_dim.11), calls=%async_computation.2 | async-start | bytes 3735552 | tf_op jit(solution)/shard_map/all_to_all | solution.py:44
  253.2 39.1 %collective-permute-done.3 = f32[1]{0:T(128)} collective-permute-done((f32[1]{0:T(128)}, f32[1]{0:T(128)}, u32[]{:S(2)}, u32[]{:S(2)}) %collective-permute-start.3) | collective-permute-done | bytes 36 | tf_op jit(solution)/shard_map/ppermute | solution.py:14
  293.0 1.4 collective-permute-start.4
  294.4 6.6 %collective-permute-done.4 = f32[1]{0:T(128)} collective-permute-done((f32[1]{0:T(128)}, f32[1]{0:T(128)}, u32[]{:S(2)}, u32[]{:S(2)}) %collective-permute-start.4) | collective-permute-done | bytes 36 | tf_op jit(solution)/shard_map/ppermute | solution.py:14
  301.6 1.4 collective-permute-start.5
  303.0 6.9 %collective-permute-done.5 = f32[1]{0:T(128)} collective-permute-done((f32[1]{0:T(128)}, f32[1]{0:T(128)}, u32[]{:S(2)}, u32[]{:S(2)}) %collective-permute-start.5) | collective-permute-done | bytes 36 | tf_op jit(solution)/shard_map/ppermute | solution.py:14
  311.0 6.7 %all_to_all.33 = f32[2,64,7169]{2,1,0:T(8,128)S(1)} all-to-all(f32[2,64,7169]{2,1,0:T(8,128)S(1)} %broadcast_in_dim.13), channel_id=1, replica_groups=mesh['node_0'=2,'node_1'=8,'node_2'=4,'node_3'=2,'blk'=2] {'node_3'}, dimensions={0} | all-to-all | bytes 7341056 | tf_op jit(solution)/shard_map/all_to_all | solution.py:44
  317.7 4.8 %copy.11 = f32[64,2,7169]{2,1,0:T(2,128)} copy(f32[64,2,7169]{2,0,1:T(8,128)S(1)} %bitcast.19) | data formatting | bytes 7341056 | tf_op jit(solution)/shard_map/transpose | solution.py:58
  322.5 6.9 %reshape_reshape.7 = f32[917632]{0:T(1024)} reshape(f32[64,2,7169]{2,1,0:T(2,128)} %copy.11) | data formatting | bytes 7341056 | tf_op jit(solution)/shard_map/reshape;reshape | solution.py:52
  329.4 1.2 slice.12
  330.6 4.8 %slice_divide_fusion = f32[917504]{0:T(1024)} fusion(f32[917632]{0:T(1024)} %reshape_reshape.7, f32[]{:T(128)} %bitcast.4), kind=kLoop, calls=%fused_computation | loop fusion | flops 917504 | bytes 7340036 | tf_op jit(solution)/shard_map/div | solution.py:105
  335.4 4.6 %div.29 = f32[64,14336]{1,0:T(8,128)} reshape(f32[917504]{0:T(1024)} %slice_divide_fusion) | data formatting | bytes 7340032 | tf_op jit(solution)/shard_map/div | solution.py:105
  340.0 48.3 %collective-permute-done.2 = f32[1,64,14336]{2,1,0:T(8,128)} collective-permute-done((f32[1,64,14336]{2,1,0:T(8,128)}, f32[1,64,14336]{2,1,0:T(8,128)}, u32[]{:S(2)}, u32[]{:S(2)}) %collective-permute-start.2) | collective-permute-done | bytes 3670048 | tf_op jit(solution)/shard_map/ppermute | solution.py:14
  388.3 7.5 %fusion.1 = (f32[]{:T(128)}, f32[1,64,14336]{2,1,0:T(8,128)}) fusion(f32[64,14336]{1,0:T(8,128)} %div.29, f32[]{:T(128)} %bitcast.1, f32[1,64,14336]{2,1,0:T(8,128)} %get-tuple-element.5, f32[1,64,14336]{2,1,0:T(8,128)} %collective-permute-done.2), kind=kLoop, calls=%fused_computation.3 | loop fusion | flops 5505023 | bytes 14680072 | tf_op jit(solution)/shard_map/reduce_sum | solution.py:106
  395.8 1.2 broadcast_in_dim.28
  397.0 3.4 all-to-all-start.4
  400.4 1.5 constant_dynamic-slice_fusion
  401.9 3.8 all-to-all-done.4
  (12 shorter events, 2.7 us)
Async XLA Ops:
  0.6 50.9 %copy-start = (bf16[1,64,14336]{2,1,0:T(8,128)(2,1)S(1)}, bf16[1,64,14336]{2,1,0:T(8,128)(2,1)}, u32[]{:S(2)}) copy-start(bf16[1,64,14336]{2,1,0:T(8,128)(2,1)} %param.2) | copy-start | bytes 5505028
  3.2 48.4 %collective-permute-start = (f32[1,64,14336]{2,1,0:T(8,128)S(1)}, f32[1,64,14336]{2,1,0:T(8,128)S(1)}, u32[]{:S(2)}, u32[]{:S(2)}) collective-permute-start(f32[1,64,14336]{2,1,0:T(8,128)S(1)} %convert_multiply_fusion), channel_id=1, source_target_pairs={{0,2},{2,4},{4,6},{6,8},{8,10},{10,12},{12,14},{14,16},{16,18},{18... | collective-permute-start | bytes 11010056 | tf_op jit(solution)/shard_map/ppermute | solution.py:14
  52.0 79.2 %collective-permute-start.1 = (f32[1,64,14336]{2,1,0:T(8,128)S(1)}, f32[1,64,14336]{2,1,0:T(8,128)S(1)}, u32[]{:S(2)}, u32[]{:S(2)}) collective-permute-start(f32[1,64,14336]{2,1,0:T(8,128)S(1)} %broadcast_multiply_fusion), channel_id=1, source_target_pairs={{0,4},{2,6},{4,8},{6,10},{8,12},{10,14},{12,16},{14,18},{16,20},{1... | collective-permute-start | bytes 11010056 | tf_op jit(solution)/shard_map/ppermute | solution.py:14
  244.4 66.2 %all-to-all-start.2 = ((f32[64,1,7169]{2,1,0:T(1,128)}), f32[64,1,7169]{2,1,0:T(1,128)S(1)}, u32[]{:S(2)}, u32[]{:S(2)}) async-start(f32[64,1,7169]{2,1,0:T(1,128)} %broadcast_in_dim.11), calls=%async_computation.2 | async-start | bytes 3735552 | tf_op jit(solution)/shard_map/all_to_all | solution.py:44
  252.2 40.1 %collective-permute-start.3 = (f32[1]{0:T(128)}, f32[1]{0:T(128)}, u32[]{:S(2)}, u32[]{:S(2)}) collective-permute-start(f32[1]{0:T(128)} %convert_element_type.6), channel_id=1, source_target_pairs={{0,2},{2,4},{4,6},{6,8},{8,10},{10,12},{12,14},{14,16},{16,18},{18... | collective-permute-start | bytes 20 | tf_op jit(solution)/shard_map/ppermute | solution.py:14
  293.0 8.0 %collective-permute-start.4 = (f32[1]{0:T(128)}, f32[1]{0:T(128)}, u32[]{:S(2)}, u32[]{:S(2)}) collective-permute-start(f32[1]{0:T(128)} %add.37), channel_id=1, source_target_pairs={{0,4},{2,6},{4,8},{6,10},{8,12},{10,14},{12,16},{14,18},{16,20},{1... | collective-permute-start | bytes 20 | tf_op jit(solution)/shard_map/ppermute | solution.py:14
  301.6 8.3 %collective-permute-start.5 = (f32[1]{0:T(128)}, f32[1]{0:T(128)}, u32[]{:S(2)}, u32[]{:S(2)}) collective-permute-start(f32[1]{0:T(128)} %add.38), channel_id=1, source_target_pairs={{0,8},{2,10},{4,12},{6,14},{8,16},{10,18},{12,20},{14,22},{16,24},... | collective-permute-start | bytes 20 | tf_op jit(solution)/shard_map/ppermute | solution.py:14
  310.5 77.8 %collective-permute-start.2 = (f32[1,64,14336]{2,1,0:T(8,128)}, f32[1,64,14336]{2,1,0:T(8,128)}, u32[]{:S(2)}, u32[]{:S(2)}) collective-permute-start(f32[1,64,14336]{2,1,0:T(8,128)} %get-tuple-element.5), channel_id=1, source_target_pairs={{0,8},{2,10},{4,12},{6,14},{8,16},{10,18},{12,20},{14,22},{16,24},... | collective-permute-start | bytes 11010056 | tf_op jit(solution)/shard_map/ppermute | solution.py:14
  397.0 8.7 %all-to-all-start.4 = ((f32[2,1,1]{2,1,0:T(1,128)}), f32[2,1,1]{2,1,0:T(1,128)S(1)}, u32[]{:S(2)}, u32[]{:S(2)}) async-start(f32[2,1,1]{2,1,0:T(1,128)} %broadcast_in_dim.28), calls=%async_computation.4 | async-start | bytes 2048 | tf_op jit(solution)/shard_map/all_to_all | solution.py:44
where the time goes:
time: 411 us; the launch traced here: 408 us
  waiting for transfers between devices  232 us (56%)
  blocking collectives  68.2 us (17%)
  local copies, waits for them, and re-layouts  65.9 us (16%)
  other arithmetic  21.5 us (5%)
  starting transfers between devices  15.2 us (4%)
  between operations  5.22 us (1%)
    ppermute x6, waiting for transfers between devices, from_behind(): return lax.ppermute(value, axis, pairs)  228 us
    all_to_all x1, blocking collectives, sum_by_axis(): return jnp.sum(lax.all_to_all(own, far, 0, 0, tiled=True), axis=0)  53.7 us
    concatenate x1, local copies, waits for them, and re-layouts, padded_to(): jnp.concatenate([lines, jnp.zeros((spare, *lines.shape[1:]), lines.dtype)])  29.5 us
    all_to_all x2, starting transfers between devices, sent_to_all(): lax.all_to_all(jnp.broadcast_to(value[None], (size, *value.shape)), axis,...  11.2 us
  transfers between devices with their start and end apart: 8, of which 7 were waited for; matrix products, arithmetic and copies ran while one was open for 6% of the time, Pallas kernels for 0%

commit v1 on v0

v1 whole, which is shorter than its diff:
```python
import jax
import jax.numpy as jnp
from jax import lax
from jax.experimental import pallas as pl
from jax.experimental.pallas import tpu as pltpu
from jax.sharding import Mesh
from jax.sharding import PartitionSpec as P

NODE = ("xl", "z", "y", "core")
RING = ("y", "core")
BLOCKS = ("xl", "z")
LANES = 128
F32 = jnp.float32


def to_all(value, axes):
    return lax.all_to_all(value, axes, 0, 0, tiled=True)


def column(ref, k):
    return ref[k, :, 0:1].astype(F32)


def block_sums_body(a_ref, b_ref, w_ref, out_ref):
    step = pl.program_id(0)
    count, nodes = out_ref.shape[0], a_ref.shape[0]
    width = a_ref.shape[2] // count
    w = [column(w_ref, k) for k in range(nodes)]
    total = sum(w[1:], w[0])

    def fill(ref):
        for q in range(count):
            at = slice(q * width, (q + 1) * width)
            acc = w[0] * ref[0, :, at].astype(F32)
            for k in range(1, nodes):
                acc = acc + w[k] * ref[k, :, at].astype(F32)
            out_ref[q, :, :width] = acc
            out_ref[q, :, width:] = jnp.broadcast_to(total, (acc.shape[0], LANES))

    half = pl.num_programs(0) // 2

    @pl.when(step < half)
    def _():
        fill(a_ref)

    @pl.when(step >= half)
    def _():
        fill(b_ref)


def block_sums(a, b, width, blocks):
    nodes, rows, cols = b.shape
    count = 4
    half = blocks // count // 2
    return pl.pallas_call(
        block_sums_body,
        grid=(2 * half,),
        in_specs=[
            pl.BlockSpec((nodes, rows, count * width), lambda s: (0, 0, jnp.minimum(s, half - 1))),
            pl.BlockSpec((nodes, rows, count * width), lambda s: (0, 0, jnp.maximum(s - half, 0))),
            pl.BlockSpec((nodes, rows, LANES), lambda s: (0, 0, cols // LANES)),
        ],
        out_specs=pl.BlockSpec((count, rows, width + LANES), lambda s: (s, 0, 0)),
        out_shape=jax.ShapeDtypeStruct((blocks, rows, width + LANES), F32),
        name="block_sums",
    )(a, b, a)


def weighted(ref, w, k):
    return w[k] * ref[k].astype(F32)


def chip_sums_body(own_ref, prev_ref, w_ref, v_ref, out_ref):
    nodes = own_ref.shape[0]
    w = [column(w_ref, k) for k in range(nodes)]
    v = [column(v_ref, k) for k in range(nodes - 1)]
    chips = nodes // 2
    after = [None] * chips
    for y in range(chips - 1, 0, -1):
        pair = weighted(prev_ref, v, 2 * y - 1) + weighted(prev_ref, v, 2 * y)
        after[y - 1] = pair if after[y] is None else after[y] + pair
    before = None
    for y in range(chips):
        parts = [part for part in (before, after[y]) if part is not None]
        out_ref[y] = sum(parts[1:], parts[0])
        if y < chips - 1:
            pair = weighted(own_ref, w, 2 * y) + weighted(own_ref, w, 2 * y + 1)
            before = pair if before is None else before + pair


def chip_sums(own, prev, w_from, v_from, cols):
    nodes, rows = own.shape[:2]
    width = cols // 4
    return pl.pallas_call(
        chip_sums_body,
        grid=(4,),
        in_specs=[
            pl.BlockSpec((nodes, rows, width), lambda s: (0, 0, s)),
            pl.BlockSpec((nodes - 1, rows, width), lambda s: (0, 0, s)),
            pl.BlockSpec((nodes, rows, LANES), lambda s: (0, 0, cols // LANES)),
            pl.BlockSpec((nodes - 1, rows, LANES), lambda s: (0, 0, cols // LANES)),
        ],
        out_specs=pl.BlockSpec((nodes // 2, rows, width), lambda s: (0, 0, s)),
        out_shape=jax.ShapeDtypeStruct((nodes // 2, rows, cols), F32),
        name="chip_sums",
    )(own, prev, w_from, v_from)


def deviations_body(own_ref, prev_ref, w_ref, v_ref, average_ref, out_ref):
    nodes = own_ref.shape[0]
    w = [column(w_ref, k) for k in range(nodes)]
    v = [column(v_ref, k) for k in range(nodes - 1)]
    average = jnp.concatenate([average_ref[q] for q in range(average_ref.shape[0])], axis=1)
    after, weight_after = [None] * nodes, [None] * nodes
    for c in range(nodes - 1, 0, -1):
        term = weighted(prev_ref, v, c - 1)
        after[c - 1] = term if after[c] is None else after[c] + term
        weight_after[c - 1] = v[c - 1] if after[c] is None else weight_after[c] + v[c - 1]
    before, weight = None, None

    @pl.when(pl.program_id(0) == 0)
    def _():
        out_ref[...] = jnp.zeros(out_ref.shape, F32)

    for c in range(nodes):
        term = weighted(own_ref, w, c)
        before = term if before is None else before + term
        weight = w[c] if weight is None else weight + w[c]
        value, scale = before, weight
        if after[c] is not None:
            value, scale = value + after[c], scale + weight_after[c]
        gap = value * (1.0 / scale) - average
        square = gap * gap
        acc = square[:, :LANES]
        for t in range(1, square.shape[1] // LANES):
            acc = acc + square[:, t * LANES : (t + 1) * LANES]
        out_ref[c] += acc


def deviations(own, prev, w_from, v_from, average, first, cols):
    nodes, rows = own.shape[:2]
    piece = average.shape[2]
    count = 2
    width = count * piece
    return pl.pallas_call(
        deviations_body,
        grid=(cols // width,),
        in_specs=[
            pl.BlockSpec((nodes, rows, width), lambda s: (0, 0, s)),
            pl.BlockSpec((nodes - 1, rows, width), lambda s: (0, 0, s)),
            pl.BlockSpec((nodes, rows, LANES), lambda s: (0, 0, cols // LANES)),
            pl.BlockSpec((nodes - 1, rows, LANES), lambda s: (0, 0, cols // LANES)),
            pl.BlockSpec((count, rows, piece), lambda s: (first // count + s, 0, 0)),
        ],
        out_specs=pl.BlockSpec((nodes, rows, LANES), lambda s: (0, 0, 0)),
        out_shape=jax.ShapeDtypeStruct((nodes, rows, LANES), F32),
        name="deviations",
    )(own, prev, w_from, v_from, average)


def debias_body(at_ref, p_ref, o_ref, same_ref, swap_ref, w_ref, v_ref, *rest):
    out_ref = rest[-1]
    c = at_ref[0]
    core = c % 2
    nodes, rows = w_ref.shape[:2]
    w = [column(w_ref, k) for k in range(nodes)]
    v = [None] + [column(v_ref, k) for k in range(nodes - 1)]
    scale = own = w[0]
    other = w[0]
    for k in range(1, nodes):
        scale = scale + jnp.where(k <= c, w[k], v[k])
        own = jnp.where(k == c, w[k], own)
        if k % 2:
            other = jnp.where(k == c + 1, v[k], other)
        else:
            other = jnp.where(k == c - 1, w[k], other)
    inverse = 1.0 / scale
    own, other = own * inverse, other * inverse
    same, swap = same_ref[0] * inverse, swap_ref[0] * inverse
    first = jnp.where(core == 0, same, swap)
    second = jnp.where(core == 0, swap, same)
    for at, total in ((slice(0, rows), first), (slice(rows, 2 * rows), second)):
        out_ref[at] = total + own * p_ref[at].astype(F32) + other * o_ref[at].astype(F32)


def debias(at, p, o, same, swap, w_from, v_from, chunk, cols, so_far):
    rows = same.shape[1]
    nodes = w_from.shape[0]
    split = 2
    width = cols // split
    wide = lambda y, s, at: (y, chunk * split + s)
    in_specs = [
        pl.BlockSpec((2 * rows, width), wide),
        pl.BlockSpec((2 * rows, width), wide),
        pl.BlockSpec((1, rows, width), lambda y, s, at: (y, 0, s)),
        pl.BlockSpec((1, rows, width), lambda y, s, at: (y, 0, s)),
        pl.BlockSpec((nodes, rows, LANES), lambda y, s, at: (0, 0, cols // LANES)),
        pl.BlockSpec((nodes - 1, rows, LANES), lambda y, s, at: (0, 0, cols // LANES)),
    ]
    operands = [at, p, o, same, swap, w_from, v_from]
    aliases = {}
    if so_far is not None:
        in_specs.append(pl.BlockSpec(memory_space=pl.ANY))
        operands.append(so_far)
        aliases = {len(operands) - 1: 0}
    return pl.pallas_call(
        debias_body,
        grid_spec=pltpu.PrefetchScalarGridSpec(
            num_scalar_prefetch=1,
            grid=(same.shape[0], split),
            in_specs=in_specs,
            out_specs=pl.BlockSpec((2 * rows, width), wide),
        ),
        out_shape=jax.ShapeDtypeStruct(p.shape, F32),
        input_output_aliases=aliases,
        name="debias",
    )(*operands)


def shards(params, weights):
    p = params[0]
    node_count = lax.axis_size(NODE)
    nodes = lax.axis_size(RING)
    blocks = lax.axis_size(BLOCKS)
    rows_all, hidden = p.shape
    rows = rows_all // nodes
    cols = hidden // 2
    width = hidden // blocks

    def moved(value, where):
        return lax.ppermute(value, NODE, [(i, where(i) % node_count) for i in range(node_count)])

    near = moved(p, lambda i: i + 1 if i % 2 == 0 else i + nodes - 1)
    weight = jnp.broadcast_to(weights.astype(p.dtype)[0], (rows_all, LANES))
    chunks = [jnp.concatenate([p[:, :cols], weight], axis=1), p[:, cols:]]
    own = [to_all(chunk.reshape(nodes, rows, -1), RING) for chunk in chunks]
    prev = [moved(piece[1:], lambda i: i + nodes) for piece in own]

    pieces = to_all(block_sums(own[0], own[1], width, blocks), BLOCKS)
    summed = jnp.sum(pieces, axis=0)
    mean = summed[:, :width] / summed[:, width : width + 1]
    means = to_all(jnp.broadcast_to(mean[None], (blocks, rows, width)), BLOCKS)
    mine = mean.reshape(rows, nodes, width // nodes).swapaxes(0, 1)
    average = to_all(mine, RING).reshape(rows_all, width // nodes)

    at = lax.axis_index(RING).astype(jnp.int32).reshape(1)
    debiased = None
    for k in range(2):
        totals = chip_sums(own[k], prev[k], own[0], prev[0], cols)
        same = to_all(totals, "y")
        swap = lax.ppermute(same, "core", [(0, 1), (1, 0)])
        debiased = debias(at, p, near, same, swap, own[0], prev[0], k, cols, debiased)

    parts = sum(
        deviations(own[k], prev[k], own[0], prev[0], means, k * blocks // 2, cols) for k in range(2)
    )
    parts = jnp.sum(parts, axis=(1, 2))
    splits = lax.axis_size("blk")
    sent = jnp.broadcast_to(parts[:, None], (nodes, splits)).reshape(nodes * splits, 1)
    spread = jnp.sum(to_all(sent, (*RING, "blk")), axis=0) / (rows_all * splits * hidden)
    return debiased[None], average, spread


def solution(mesh):
    finer = Mesh(
        mesh.devices.reshape(2, 8, 4, 2, mesh.shape["blk"]),
        (*NODE, "blk"),
    )
    return jax.shard_map(
        shards,
        mesh=finer,
        in_specs=(P(NODE, "blk", None), P(NODE)),
        out_specs=(P(NODE, "blk", None), P("blk", NODE), P(NODE)),
        check_vma=False,
    )
```

time: 411 us -> 189 us (0.46)
  waiting for transfers between devices: 232 us -> 77.5 us
  local copies, waits for them, and re-layouts: 65.9 us -> 8.04 us
  blocking collectives: 68.2 us -> 19 us
  Pallas kernels: 0 us -> 32.2 us
  starting transfers between devices: 15.2 us -> 42.2 us
  other arithmetic: 21.5 us -> 3.75 us
    ppermute x6 -> x5, waiting for transfers between devices: 228 us -> 36.7 us  [the longest x3 36.7 us: moved(): lax.ppermute(value, NODE, [(i, where(i) % node_count) for i in range(node...]
    all_to_all x3 -> x1, blocking collectives: 68.2 us -> 19 us  [to_all(): return lax.all_to_all(value, axes, 0, 0, tiled=True)]
    all_to_all x2 -> x7, waiting for transfers between devices: 3.75 us -> 40.9 us  [to_all(): return lax.all_to_all(value, axes, 0, 0, tiled=True)]
    pallas_call x0 -> x7, Pallas kernels: none -> 32.2 us  [the longest x2 13.1 us: debias(): pl.pallas_call(debias_body, grid_spec=pltpu.PrefetchScalarGridSpec(num_sc...]
    concatenate x1 -> x0, local copies, waits for them, and re-layouts: 29.5 us -> none  [padded_to(): jnp.concatenate([lines, jnp.zeros((spare, *lines.shape[1:]), lines.dtype)])]
    all_to_all x2 -> x7, starting transfers between devices: 11.2 us -> 38.6 us  [to_all(): return lax.all_to_all(value, axes, 0, 0, tiled=True)]
    another operation x2 -> x0, local copies, waits for them, and re-layouts: 14.4 us -> none  [the longest x1 7.56 us: cut_along(): value.reshape(*lengths[:dim], size, lengths[dim] // size, *lengths[dim +...]
    reduce_sum x4 -> x3, other arithmetic: 11.7 us -> 2.59 us  [the longest x1 1.08 us: shards(): summed = jnp.sum(pieces, axis=0)]
  transfers between devices with their start and end apart: 8 -> 12, of which waited for: 7 -> 7; matrix products, arithmetic and copies ran while one was open for 6% -> 3% of each run, Pallas kernels for 0% -> 12%
where the time goes in v1:
time: 189 us; the launch traced here: 186 us
  waiting for transfers between devices  77.5 us (41%)
  starting transfers between devices  42.2 us (22%)
  Pallas kernels  32.2 us (17%)
  blocking collectives  19 us (10%)
  local copies, waits for them, and re-layouts  8.04 us (4%)
  other arithmetic  3.75 us (2%)
  between operations  3.23 us (2%)
    all_to_all x7, waiting for transfers between devices, to_all(): return lax.all_to_all(value, axes, 0, 0, tiled=True)  40.9 us
    all_to_all x7, starting transfers between devices, to_all(): return lax.all_to_all(value, axes, 0, 0, tiled=True)  38.6 us
    ppermute x3, waiting for transfers between devices, moved(): lax.ppermute(value, NODE, [(i, where(i) % node_count) for i in range(node...  36.7 us
    all_to_all x1, blocking collectives, to_all(): return lax.all_to_all(value, axes, 0, 0, tiled=True)  19 us
    pallas_call x2, Pallas kernels, debias(): pl.pallas_call(debias_body, grid_spec=pltpu.PrefetchScalarGridSpec(num_sc...  13.1 us
    pallas_call x2, Pallas kernels, chip_sums(): pl.pallas_call(chip_sums_body, grid=(4,), in_specs=[pl.BlockSpec((nodes,...  7.58 us
    pallas_call x2, Pallas kernels, deviations(): pl.pallas_call(deviations_body, grid=(cols // width,), in_specs=[pl.Block...  7.48 us
    pallas_call x1, Pallas kernels, block_sums(): pl.pallas_call(block_sums_body, grid=(2 * half,), in_specs=[pl.BlockSpec(...  3.96 us
  transfers between devices with their start and end apart: 12, of which 7 were waited for; matrix products, arithmetic and copies ran while one was open for 3% of the time, Pallas kernels for 12%

profile of v1, /device:TPU:2, one launch (start us, length us, event | category | flops | bytes accessed | tf_op | source)
XLA Modules:
  0.0 185.9 jit_solution(4509873818964894889)
XLA Ops:
  0.7 2.3 %slice_bitcast_fusion = bf16[8,8,7168]{2,1,0:T(8,128)(2,1)} fusion(bf16[64,14336]{1,0:T(8,128)(2,1)} %bitcast.13), kind=kLoop, calls=%fused_computation.2 | loop fusion | bytes 1835008 | tf_op jit(solution)/shard_map/reshape | solution.py:236
  3.0 4.5 %all-to-all-start = ((bf16[8,8,7168]{2,1,0:T(8,128)(2,1)}), bf16[8,8,7168]{2,1,0:T(8,128)(2,1)S(1)}, u32[]{:S(2)}, u32[]{:S(2)}) async-start(bf16[8,8,7168]{2,1,0:T(8,128)(2,1)} %slice_bitcast_fusion), calls=%async_computation | async-start | bytes 1835008 | tf_op jit(solution)/shard_map/all_to_all | solution.py:17
  8.1 1.1 fusion
  9.2 12.8 %all-to-all-done.own_ref.b_ref = bf16[8,8,7168]{2,1,0:T(8,128)(2,1)S(1)} async-done(((bf16[8,8,7168]{2,1,0:T(8,128)(2,1)}), bf16[8,8,7168]{2,1,0:T(8,128)(2,1)S(1)}, u32[]{:S(2)}, u32[]{:S(2)}) %all-to-all-start) | async-done | bytes 917536 | tf_op jit(solution)/shard_map/all_to_all | solution.py:17
  22.0 19.0 %all_to_all.45.w_ref.own_ref.a_ref = bf16[8,8,7296]{2,1,0:T(8,128)(2,1)} all-to-all(bf16[8,8,7296]{2,1,0:T(8,128)(2,1)} %fusion), channel_id=1, replica_groups=mesh['xl'=2,'z'=8,'y'=4,'core'=2,'blk'=2] {'y','core'}, dimensions={0} | all-to-all | bytes 1867776 | tf_op jit(solution)/shard_map/all_to_all | solution.py:17
  40.9 4.0 %block_sums.1 = f32[16,8,1024]{2,1,0:T(8,128)} custom-call(bf16[8,8,7296]{2,1,0:T(8,128)(2,1)} %all_to_all.45.w_ref.own_ref.a_ref, bf16[8,8,7168]{2,1,0:T(8,128)(2,1)} %copy-done.2, bf16[8,8,7296]{2,1,0:T(8,128)(2,1)} %all_to_all.45.w_ref.own_ref.a_ref), custom_call_target="tpu_custom_call" | custom-call | tf_op jit(solution)/shard_map/block_sums/pallas_call | solution.py:55
  44.9 10.1 %all-to-all-start.4 = ((f32[16,8,1024]{2,1,0:T(8,128)}), f32[16,8,1024]{2,1,0:T(8,128)S(1)}, u32[]{:S(2)}, u32[]{:S(2)}) async-start(f32[16,8,1024]{2,1,0:T(8,128)} %block_sums.1), calls=%async_computation.4 | async-start | bytes 1048576 | tf_op jit(solution)/shard_map/all_to_all | solution.py:17
  55.0 1.5 collective-permute-start.2
  56.6 0.9 slice.26
  57.5 1.5 collective-permute-start.1
  59.0 28.5 %collective-permute-done.2.v_ref.prev_ref = bf16[7,8,7296]{2,1,0:T(8,128)(2,1)S(1)} collective-permute-done((bf16[7,8,7296]{2,1,0:T(8,128)(2,1)S(1)}, bf16[7,8,7296]{2,1,0:T(8,128)(2,1)S(1)}, u32[]{:S(2)}, u32[]{:S(2)}) %collective-permute-start.2) | collective-permute-done | bytes 817184 | tf_op jit(solution)/shard_map/ppermute | solution.py:231
  87.5 0.9 copy-done.1
  88.4 3.8 %chip_sums.3 = f32[4,8,7168]{2,1,0:T(8,128)} custom-call(bf16[8,8,7296]{2,1,0:T(8,128)(2,1)} %all_to_all.45.w_ref.own_ref.a_ref, bf16[7,8,7296]{2,1,0:T(8,128)(2,1)} %copy-done.1, bf16[8,8,7296]{2,1,0:T(8,128)(2,1)} %all_to_all.45.w_ref.own_ref.a_ref, bf16[7,8,7296]{2,1,0:T(8,128)(2,1)} %copy-done.1), custom_call_target="tpu_custom_call" | custom-call | tf_op jit(solution)/shard_map/chip_sums/pallas_call | solution.py:94
  92.2 0.8 copy-done.8
  93.0 3.5 %all-to-all-start.3 = ((f32[4,8,7168]{2,1,0:T(8,128)}), f32[4,8,7168]{2,1,0:T(8,128)S(1)}, u32[]{:S(2)}, u32[]{:S(2)}) async-start(f32[4,8,7168]{2,1,0:T(8,128)} %chip_sums.3), calls=%async_computation.3 | async-start | bytes 1835008 | tf_op jit(solution)/shard_map/all_to_all | solution.py:17
  96.6 8.2 %collective-permute-done.1.prev_ref = bf16[7,8,7168]{2,1,0:T(8,128)(2,1)} collective-permute-done((bf16[7,8,7168]{2,1,0:T(8,128)(2,1)}, bf16[7,8,7168]{2,1,0:T(8,128)(2,1)}, u32[]{:S(2)}, u32[]{:S(2)}) %collective-permute-start.1) | collective-permute-done | bytes 802848 | tf_op jit(solution)/shard_map/ppermute | solution.py:231
  104.8 3.8 %chip_sums.2 = f32[4,8,7168]{2,1,0:T(8,128)} custom-call(bf16[8,8,7168]{2,1,0:T(8,128)(2,1)} %copy-done.2, bf16[7,8,7168]{2,1,0:T(8,128)(2,1)} %collective-permute-done.1.prev_ref, bf16[8,8,7296]{2,1,0:T(8,128)(2,1)} %all_to_all.45.w_ref.own_ref.a_ref, bf16[7,8,7296]{2,1,0:T(8,128)(2,1)} %copy-done.1), custom_call_target="tpu_custom_call" | custom-call | tf_op jit(solution)/shard_map/chip_sums/pallas_call | solution.py:94
  108.8 4.2 %all-to-all-start.2 = ((f32[4,8,7168]{2,1,0:T(8,128)}), f32[4,8,7168]{2,1,0:T(8,128)}, u32[]{:S(2)}, u32[]{:S(2)}) async-start(f32[4,8,7168]{2,1,0:T(8,128)} %chip_sums.2), calls=%async_computation.2 | async-start | bytes 1835008 | tf_op jit(solution)/shard_map/all_to_all | solution.py:17
  113.0 1.1 reduce_sum.27
  114.3 10.9 %all-to-all-done.2.same_ref = f32[4,8,7168]{2,1,0:T(8,128)} async-done(((f32[4,8,7168]{2,1,0:T(8,128)}), f32[4,8,7168]{2,1,0:T(8,128)}, u32[]{:S(2)}, u32[]{:S(2)}) %all-to-all-start.2) | async-done | bytes 917536 | tf_op jit(solution)/shard_map/all_to_all | solution.py:17
  125.2 0.8 broadcast_in_dim.7
  126.0 6.6 %all-to-all-start.6 = ((f32[16,8,896]{2,1,0:T(8,128)}), f32[16,8,896]{2,1,0:T(8,128)S(1)}, u32[]{:S(2)}, u32[]{:S(2)}) async-start(f32[16,8,896]{2,1,0:T(8,128)} %broadcast_in_dim.7), calls=%async_computation.6 | async-start | bytes 917504 | tf_op jit(solution)/shard_map/all_to_all | solution.py:17
  133.8 9.5 %all-to-all-done.6.average_ref = f32[16,8,896]{2,1,0:T(8,128)S(1)} async-done(((f32[16,8,896]{2,1,0:T(8,128)}), f32[16,8,896]{2,1,0:T(8,128)S(1)}, u32[]{:S(2)}, u32[]{:S(2)}) %all-to-all-start.6) | async-done | bytes 458784 | tf_op jit(solution)/shard_map/all_to_all | solution.py:17
  143.4 3.3 %all-to-all-start.5 = ((f32[8,8,112]{2,1,0:T(8,128)}), f32[8,8,112]{2,1,0:T(8,128)S(1)}, u32[]{:S(2)}, u32[]{:S(2)}) async-start(f32[8,8,112]{2,1,0:T(8,128)} %bitcast.12), calls=%async_computation.5 | async-start | bytes 65536 | tf_op jit(solution)/shard_map/all_to_all | solution.py:17
  146.7 3.7 %deviations.3 = f32[8,8,128]{2,1,0:T(8,128)} custom-call(bf16[8,8,7168]{2,1,0:T(8,128)(2,1)} %copy-done.2, bf16[7,8,7168]{2,1,0:T(8,128)(2,1)} %collective-permute-done.1.prev_ref, bf16[8,8,7296]{2,1,0:T(8,128)(2,1)} %all_to_all.45.w_ref.own_ref.a_ref, bf16[7,8,7296]{2,1,0:T(8,128)(2,1)} %copy-done.1, f32[16,8,896]{2,1,0:T(8,128)} %copy-done.6), custom_call_target="tpu_custom_call" | custom-call | tf_op jit(solution)/shard_map/deviations/pallas_call | solution.py:145
  150.5 3.7 %deviations.2 = f32[8,8,128]{2,1,0:T(8,128)} custom-call(bf16[8,8,7296]{2,1,0:T(8,128)(2,1)} %all_to_all.45.w_ref.own_ref.a_ref, bf16[7,8,7296]{2,1,0:T(8,128)(2,1)} %copy-done.1, bf16[8,8,7296]{2,1,0:T(8,128)(2,1)} %all_to_all.45.w_ref.own_ref.a_ref, bf16[7,8,7296]{2,1,0:T(8,128)(2,1)} %copy-done.1, f32[16,8,896]{2,1,0:T(8,128)} %copy-done.6), custom_call_target="tpu_custom_call" | custom-call | tf_op jit(solution)/shard_map/deviations/pallas_call | solution.py:145
  154.2 0.9 add_reduce_fusion
  155.2 0.7 all_to_all.36
  155.9 6.4 %all-to-all-start.7 = ((f32[16,1,1]{2,1,0:T(1,128)}), f32[16,1,1]{2,1,0:T(1,128)S(1)}, u32[]{:S(2)}, u32[]{:S(2)}) async-start(f32[16,1,1]{2,1,0:T(1,128)} %all_to_all.36), calls=%async_computation.7 | async-start | bytes 16384 | tf_op jit(solution)/shard_map/all_to_all | solution.py:17
  162.2 7.5 %all-to-all-done.7 = f32[16,1,1]{2,1,0:T(1,128)S(1)} async-done(((f32[16,1,1]{2,1,0:T(1,128)}), f32[16,1,1]{2,1,0:T(1,128)S(1)}, u32[]{:S(2)}, u32[]{:S(2)}) %all-to-all-start.7) | async-done | bytes 96 | tf_op jit(solution)/shard_map/all_to_all | solution.py:17
  171.1 6.6 %debias.2.rest_0_ = f32[64,14336]{1,0:T(8,128)} custom-call(s32[1]{0:T(128)} %bitcast.at_ref, bf16[64,14336]{1,0:T(8,128)(2,1)} %bitcast.14, bf16[64,14336]{1,0:T(8,128)(2,1)} %collective-permute-done.o_ref, f32[4,8,7168]{2,1,0:T(8,128)} %copy-done.7, f32[4,8,7168]{2,1,0:T(8,128)} %collective-permute-done.4.swap_ref, ...), custom_call_target="tpu_custom_call" | custom-call | tf_op jit(solution)/shard_map/debias/pallas_call | solution.py:206
  177.6 6.6 %debias.3 = f32[64,14336]{1,0:T(8,128)} custom-call(s32[1]{0:T(128)} %bitcast.at_ref, bf16[64,14336]{1,0:T(8,128)(2,1)} %bitcast.15, bf16[64,14336]{1,0:T(8,128)(2,1)} %collective-permute-done.o_ref, f32[4,8,7168]{2,1,0:T(8,128)} %all-to-all-done.2.same_ref, f32[4,8,7168]{2,1,0:T(8,128)} %collective-permute-done.3.swap_ref, ...), custom_call_target="tpu_custom_call", output_to_operand_aliasing={{}: (7, {})} | custom-call | tf_op jit(solution)/shard_map/debias/pallas_call | solution.py:206
  (37 shorter events, 3.2 us)
Async XLA Ops:
  0.6 7.5 %copy-start.4 = (bf16[1,64,14336]{2,1,0:T(8,128)(2,1)S(1)}, bf16[1,64,14336]{2,1,0:T(8,128)(2,1)}, u32[]{:S(2)}) copy-start(bf16[1,64,14336]{2,1,0:T(8,128)(2,1)} %param.2) | copy-start | bytes 5505028
  0.6 7.5 %copy-start.10 = (pred[7296]{0:T(1024)(128)(4,1)S(1)}, pred[7296]{0:T(1024)(128)(4,1)}, u32[]{:S(2)}) copy-start(pred[7296]{0:T(1024)(128)(4,1)} %constant.16.clone.1) | copy-start | bytes 21892
  3.0 19.0 %all-to-all-start = ((bf16[8,8,7168]{2,1,0:T(8,128)(2,1)}), bf16[8,8,7168]{2,1,0:T(8,128)(2,1)S(1)}, u32[]{:S(2)}, u32[]{:S(2)}) async-start(bf16[8,8,7168]{2,1,0:T(8,128)(2,1)} %slice_bitcast_fusion), calls=%async_computation | async-start | bytes 1835008 | tf_op jit(solution)/shard_map/all_to_all | solution.py:17
  22.0 19.0 %copy-start.2 = (bf16[8,8,7168]{2,1,0:T(8,128)(2,1)}, bf16[8,8,7168]{2,1,0:T(8,128)(2,1)S(1)}, u32[]{:S(2)}) copy-start(bf16[8,8,7168]{2,1,0:T(8,128)(2,1)S(1)} %all-to-all-done.own_ref.b_ref) | copy-start | bytes 2752516
  40.9 14.0 %copy-start = (bf16[8,8,7296]{2,1,0:T(8,128)(2,1)S(1)}, bf16[8,8,7296]{2,1,0:T(8,128)(2,1)}, u32[]{:S(2)}) copy-start(bf16[8,8,7296]{2,1,0:T(8,128)(2,1)} %all_to_all.45.w_ref.own_ref.a_ref) | copy-start | bytes 2801668
  44.9 11.7 %copy-start.3 = (bf16[8,8,7168]{2,1,0:T(8,128)(2,1)S(1)}, bf16[8,8,7168]{2,1,0:T(8,128)(2,1)}, u32[]{:S(2)}) copy-start(bf16[8,8,7168]{2,1,0:T(8,128)(2,1)} %copy-done.2) | copy-start | bytes 2752516
  44.9 47.3 %all-to-all-start.4 = ((f32[16,8,1024]{2,1,0:T(8,128)}), f32[16,8,1024]{2,1,0:T(8,128)S(1)}, u32[]{:S(2)}, u32[]{:S(2)}) async-start(f32[16,8,1024]{2,1,0:T(8,128)} %block_sums.1), calls=%async_computation.4 | async-start | bytes 1048576 | tf_op jit(solution)/shard_map/all_to_all | solution.py:17
  55.0 32.5 %collective-permute-start.2 = (bf16[7,8,7296]{2,1,0:T(8,128)(2,1)S(1)}, bf16[7,8,7296]{2,1,0:T(8,128)(2,1)S(1)}, u32[]{:S(2)}, u32[]{:S(2)}) collective-permute-start(bf16[7,8,7296]{2,1,0:T(8,128)(2,1)S(1)} %slice.28), channel_id=1, source_target_pairs={{0,16},{2,18},{4,20},{6,22},{8,24},{10,26},{12,28},{14,30},{16,32}... | collective-permute-start | bytes 2451464 | tf_op jit(solution)/shard_map/ppermute | solution.py:231
  57.5 47.3 %collective-permute-start.1 = (bf16[7,8,7168]{2,1,0:T(8,128)(2,1)}, bf16[7,8,7168]{2,1,0:T(8,128)(2,1)}, u32[]{:S(2)}, u32[]{:S(2)}) collective-permute-start(bf16[7,8,7168]{2,1,0:T(8,128)(2,1)} %slice.26), channel_id=1, source_target_pairs={{0,16},{2,18},{4,20},{6,22},{8,24},{10,26},{12,28},{14,30},{16,32}... | collective-permute-start | bytes 2408456 | tf_op jit(solution)/shard_map/ppermute | solution.py:231
  87.5 0.9 copy-start.1
  92.2 4.3 %copy-start.5 = (bf16[1,64,14336]{2,1,0:T(8,128)(2,1)S(1)}, bf16[1,64,14336]{2,1,0:T(8,128)(2,1)}, u32[]{:S(2)}) copy-start(bf16[1,64,14336]{2,1,0:T(8,128)(2,1)} %param.2) | copy-start | bytes 5505028
  92.2 0.8 copy-start.8
  93.0 15.7 %all-to-all-start.3 = ((f32[4,8,7168]{2,1,0:T(8,128)}), f32[4,8,7168]{2,1,0:T(8,128)S(1)}, u32[]{:S(2)}, u32[]{:S(2)}) async-start(f32[4,8,7168]{2,1,0:T(8,128)} %chip_sums.3), calls=%async_computation.3 | async-start | bytes 1835008 | tf_op jit(solution)/shard_map/all_to_all | solution.py:17
  96.6 74.5 %collective-permute-start = (bf16[64,14336]{1,0:T(8,128)(2,1)S(1)}, bf16[64,14336]{1,0:T(8,128)(2,1)}, u32[]{:S(2)}, u32[]{:S(2)}) collective-permute-start(bf16[64,14336]{1,0:T(8,128)(2,1)S(1)} %bitcast.17), channel_id=1, source_target_pairs={{0,2},{2,16},{4,6},{6,20},{8,10},{10,24},{12,14},{14,28},{16,18},{... | collective-permute-start | bytes 5505032 | tf_op jit(solution)/shard_map/ppermute | solution.py:231
  108.8 23.8 %copy-start.7 = (f32[4,8,7168]{2,1,0:T(8,128)}, f32[4,8,7168]{2,1,0:T(8,128)S(1)}, u32[]{:S(2)}) copy-start(f32[4,8,7168]{2,1,0:T(8,128)S(1)} %all-to-all-done.3.same_ref) | copy-start | bytes 2752516
  108.8 16.4 %all-to-all-start.2 = ((f32[4,8,7168]{2,1,0:T(8,128)}), f32[4,8,7168]{2,1,0:T(8,128)}, u32[]{:S(2)}, u32[]{:S(2)}) async-start(f32[4,8,7168]{2,1,0:T(8,128)} %chip_sums.2), calls=%async_computation.2 | async-start | bytes 1835008 | tf_op jit(solution)/shard_map/all_to_all | solution.py:17
  126.0 17.4 %all-to-all-start.6 = ((f32[16,8,896]{2,1,0:T(8,128)}), f32[16,8,896]{2,1,0:T(8,128)S(1)}, u32[]{:S(2)}, u32[]{:S(2)}) async-start(f32[16,8,896]{2,1,0:T(8,128)} %broadcast_in_dim.7), calls=%async_computation.6 | async-start | bytes 917504 | tf_op jit(solution)/shard_map/all_to_all | solution.py:17
  132.5 38.5 %collective-permute-start.4 = (f32[4,8,7168]{2,1,0:T(8,128)S(1)}, f32[4,8,7168]{2,1,0:T(8,128)}, u32[]{:S(2)}, u32[]{:S(2)}) collective-permute-start(f32[4,8,7168]{2,1,0:T(8,128)S(1)} %all-to-all-done.3.same_ref), channel_id=1, source_target_pairs={{0,2},{2,0},{1,3},{3,1},{4,6},{6,4},{5,7},{7,5},{8,10},{10,8},{9,1... | collective-permute-start | bytes 2752520 | tf_op jit(solution)/shard_map/ppermute | solution.py:251
  132.6 45.0 %collective-permute-start.3 = (f32[4,8,7168]{2,1,0:T(8,128)}, f32[4,8,7168]{2,1,0:T(8,128)}, u32[]{:S(2)}, u32[]{:S(2)}) collective-permute-start(f32[4,8,7168]{2,1,0:T(8,128)} %all-to-all-done.2.same_ref), channel_id=1, source_target_pairs={{0,2},{2,0},{1,3},{3,1},{4,6},{6,4},{5,7},{7,5},{8,10},{10,8},{9,1... | collective-permute-start | bytes 2752520 | tf_op jit(solution)/shard_map/ppermute | solution.py:251
  143.4 3.4 %copy-start.6 = (f32[16,8,896]{2,1,0:T(8,128)}, f32[16,8,896]{2,1,0:T(8,128)S(1)}, u32[]{:S(2)}) copy-start(f32[16,8,896]{2,1,0:T(8,128)S(1)} %all-to-all-done.6.average_ref) | copy-start | bytes 1376260
  143.4 12.5 %all-to-all-start.5 = ((f32[8,8,112]{2,1,0:T(8,128)}), f32[8,8,112]{2,1,0:T(8,128)S(1)}, u32[]{:S(2)}, u32[]{:S(2)}) async-start(f32[8,8,112]{2,1,0:T(8,128)} %bitcast.12), calls=%async_computation.5 | async-start | bytes 65536 | tf_op jit(solution)/shard_map/all_to_all | solution.py:17
  150.5 3.7 %copy-start.9 = (f32[8,8,128]{2,1,0:T(8,128)S(1)}, f32[8,8,128]{2,1,0:T(8,128)}, u32[]{:S(2)}) copy-start(f32[8,8,128]{2,1,0:T(8,128)} %deviations.3) | copy-start | bytes 98308
  155.9 13.9 %all-to-all-start.7 = ((f32[16,1,1]{2,1,0:T(1,128)}), f32[16,1,1]{2,1,0:T(1,128)S(1)}, u32[]{:S(2)}, u32[]{:S(2)}) async-start(f32[16,1,1]{2,1,0:T(1,128)} %all_to_all.36), calls=%async_computation.7 | async-start | bytes 16384 | tf_op jit(solution)/shard_map/all_to_all | solution.py:17

commit v2 on v1

v2 whole, which is shorter than its diff:
```python
import jax
import jax.numpy as jnp
from jax import lax
from jax.experimental import pallas as pl
from jax.experimental.pallas import tpu as pltpu
from jax.sharding import Mesh
from jax.sharding import PartitionSpec as P

NODE = ("xl", "z", "y", "core")
RING = ("y", "core")
BLOCKS = ("xl", "z")
CHUNKS = 2
LANES = 128
F32 = jnp.float32


def to_all(value, axes):
    return lax.all_to_all(value, axes, 0, 0, tiled=True)


def columns(ref):
    return [ref[k].astype(F32) for k in range(ref.shape[0])]


def block_sums_body(a_ref, b_ref, w_ref, out_ref):
    w = columns(w_ref)
    total = sum(w[1:], w[0])
    first_half = pl.program_id(0) < pl.num_programs(0) // 2
    for ref, chosen in ((a_ref, first_half), (b_ref, jnp.logical_not(first_half))):
        pl.when(chosen)(lambda ref=ref: fill_sums(ref, w, total, out_ref))


def fill_sums(own_ref, w, total, out_ref):
    pieces, _, wide = out_ref.shape
    width = wide - LANES
    for q in range(pieces):
        for t in range(width // LANES):
            at = slice(q * width + t * LANES, q * width + (t + 1) * LANES)
            acc = w[0] * own_ref[0, :, at].astype(F32)
            for k in range(1, len(w)):
                acc = acc + w[k] * own_ref[k, :, at].astype(F32)
            out_ref[q, :, t * LANES : (t + 1) * LANES] = acc
        out_ref[q, :, width:] = total


def spare(ref_array, cols):
    return pl.BlockSpec((*ref_array.shape[:2], LANES), lambda *_: (0, 0, cols // LANES))


def block_sums(own, width, blocks):
    nodes, rows, cols = own[1].shape
    pieces = 4
    half = blocks // pieces // 2
    block = (nodes, rows, pieces * width)
    return pl.pallas_call(
        block_sums_body,
        grid=(2 * half,),
        in_specs=[
            pl.BlockSpec(block, lambda s: (0, 0, jnp.minimum(s, half - 1))),
            pl.BlockSpec(block, lambda s: (0, 0, jnp.maximum(s - half, 0))),
            spare(own[0], cols),
        ],
        out_specs=pl.BlockSpec((pieces, rows, width + LANES), lambda s: (s, 0, 0)),
        out_shape=jax.ShapeDtypeStruct((blocks, rows, width + LANES), F32),
        name="block_sums",
    )(own[0], own[1], own[0])


def chip_sums_body(own_ref, prev_ref, w_ref, v_ref, out_ref):
    w, v = columns(w_ref), columns(v_ref)
    chips, _, width = out_ref.shape
    for t in range(width // LANES):
        at = slice(t * LANES, (t + 1) * LANES)
        after = [None] * chips
        for y in range(chips - 1, 0, -1):
            k = 2 * y
            pair = v[k - 1] * prev_ref[k - 1, :, at].astype(F32)
            pair = pair + v[k] * prev_ref[k, :, at].astype(F32)
            after[y - 1] = pair if after[y] is None else after[y] + pair
        before = None
        for y in range(chips):
            parts = [part for part in (before, after[y]) if part is not None]
            out_ref[y, :, at] = sum(parts[1:], parts[0])
            if y < chips - 1:
                k = 2 * y
                pair = w[k] * own_ref[k, :, at].astype(F32)
                pair = pair + w[k + 1] * own_ref[k + 1, :, at].astype(F32)
                before = pair if before is None else before + pair


def chip_sums(own, prev, own0, prev0, cols):
    nodes, rows = own.shape[:2]
    steps = 4
    width = cols // steps
    return pl.pallas_call(
        chip_sums_body,
        grid=(steps,),
        in_specs=[
            pl.BlockSpec((nodes, rows, width), lambda s: (0, 0, s)),
            pl.BlockSpec((nodes - 1, rows, width), lambda s: (0, 0, s)),
            spare(own0, cols),
            spare(prev0, cols),
        ],
        out_specs=pl.BlockSpec((nodes // 2, rows, width), lambda s: (0, 0, s)),
        out_shape=jax.ShapeDtypeStruct((nodes // 2, rows, cols), F32),
        name="chip_sums",
    )(own, prev, own0, prev0)


def deviations_body(*refs):
    own_refs, prev_refs = refs[:CHUNKS], refs[CHUNKS : 2 * CHUNKS]
    w_ref, v_ref, means_ref, out_ref = refs[2 * CHUNKS :]
    w, v = columns(w_ref), columns(v_ref)
    nodes = len(w)
    pieces, _, width = means_ref.shape
    inverse = []
    for c in range(nodes):
        terms = w[: c + 1] + v[c:]
        inverse.append(1.0 / sum(terms[1:], terms[0]))
    step = pl.program_id(0)

    @pl.when(step == 0)
    def _():
        out_ref[...] = jnp.zeros(out_ref.shape, F32)

    def fill(own_ref, prev_ref):
        accs = [out_ref[c] for c in range(nodes)]
        for q in range(pieces):
            for t in range(width // LANES):
                at = slice(q * width + t * LANES, q * width + (t + 1) * LANES)
                mean = means_ref[q, :, t * LANES : (t + 1) * LANES]
                after = [None] * nodes
                for c in range(nodes - 1, 0, -1):
                    term = v[c - 1] * prev_ref[c - 1, :, at].astype(F32)
                    after[c - 1] = term if after[c] is None else after[c] + term
                before = None
                for c in range(nodes):
                    term = w[c] * own_ref[c, :, at].astype(F32)
                    before = term if before is None else before + term
                    value = before if after[c] is None else before + after[c]
                    gap = value * inverse[c] - mean
                    accs[c] = accs[c] + gap * gap
        for c in range(nodes):
            out_ref[c] = accs[c]

    per = pl.num_programs(0) // CHUNKS
    for q in range(CHUNKS):
        pl.when(step // per == q)(lambda q=q: fill(own_refs[q], prev_refs[q]))


def deviations(own, prev, means, cols):
    nodes, rows = own[0].shape[:2]
    blocks, _, piece = means.shape
    pieces = 4
    steps = blocks // pieces
    per = steps // CHUNKS
    width = pieces * piece

    def near(count, q):
        return pl.BlockSpec((count, rows, width), lambda s: (0, 0, jnp.clip(s - q * per, 0, per - 1)))

    return pl.pallas_call(
        deviations_body,
        grid=(steps,),
        in_specs=[
            *[near(nodes, q) for q in range(CHUNKS)],
            *[near(nodes - 1, q) for q in range(CHUNKS)],
            spare(own[0], cols),
            spare(prev[0], cols),
            pl.BlockSpec((pieces, rows, piece), lambda s: (s, 0, 0)),
        ],
        out_specs=pl.BlockSpec((nodes, rows, LANES), lambda s: (0, 0, 0)),
        out_shape=jax.ShapeDtypeStruct((nodes, rows, LANES), F32),
        name="deviations",
    )(*own, *prev, own[0], prev[0], means)


def debias_body(at_ref, p_ref, near_ref, same_ref, swap_ref, w_ref, v_ref, *rest):
    out_ref = rest[-1]
    c = at_ref[0]
    even = c % 2 == 0
    rows = w_ref.shape[1]
    w = [value[:, 0:1] for value in columns(w_ref)]
    v = [None] + [value[:, 0:1] for value in columns(v_ref)]
    scale = own = other = w[0]
    for k in range(1, len(w)):
        scale = scale + jnp.where(k <= c, w[k], v[k])
        own = jnp.where(k == c, w[k], own)
        if k % 2:
            other = jnp.where(k == c + 1, v[k], other)
        else:
            other = jnp.where(k == c - 1, w[k], other)
    inverse = 1.0 / scale
    own, other = own * inverse, other * inverse
    same, swap = same_ref[0] * inverse, swap_ref[0] * inverse
    halves = (jnp.where(even, same, swap), jnp.where(even, swap, same))
    for half, total in enumerate(halves):
        at = slice(half * rows, (half + 1) * rows)
        out_ref[at] = total + own * p_ref[at].astype(F32) + other * near_ref[at].astype(F32)


def debias(at, p, near, same, swap, own0, prev0, chunk, so_far):
    chips, rows, cols = same.shape
    wide = pl.BlockSpec((2 * rows, cols), lambda y, at: (y, chunk))
    part = pl.BlockSpec((1, rows, cols), lambda y, at: (y, 0, 0))
    in_specs = [wide, wide, part, part, spare(own0, cols), spare(prev0, cols)]
    operands = [at, p, near, same, swap, own0, prev0]
    aliases = {}
    if so_far is not None:
        in_specs.append(pl.BlockSpec(memory_space=pl.ANY))
        operands.append(so_far)
        aliases = {len(operands) - 1: 0}
    return pl.pallas_call(
        debias_body,
        grid_spec=pltpu.PrefetchScalarGridSpec(
            num_scalar_prefetch=1,
            grid=(chips,),
            in_specs=in_specs,
            out_specs=wide,
        ),
        out_shape=jax.ShapeDtypeStruct(p.shape, F32),
        input_output_aliases=aliases,
        name="debias",
    )(*operands)


def body(params, weights):
    p = params[0]
    node_count = lax.axis_size(NODE)
    nodes = lax.axis_size(RING)
    blocks = lax.axis_size(BLOCKS)
    splits = lax.axis_size("blk")
    rows_all, hidden = p.shape
    rows = rows_all // nodes
    cols = hidden // CHUNKS
    width = hidden // blocks
    piece = width // nodes

    def moved(value, where):
        return lax.ppermute(value, NODE, [(i, where(i) % node_count) for i in range(node_count)])

    near = moved(p, lambda i: i + 1 if i % 2 == 0 else i + nodes - 1)
    weight = jnp.broadcast_to(weights.astype(p.dtype)[0], (rows_all, LANES))
    chunks = [jnp.concatenate([p[:, :cols], weight], axis=1), p[:, cols:]]
    own, prev = [], []
    for k in range(CHUNKS):
        own.append(to_all(chunks[k].reshape(nodes, rows, -1), RING))
        prev.append(moved(own[k][1:], lambda i: i + nodes))

    summed = jnp.sum(to_all(block_sums(own, width, blocks), BLOCKS), axis=0)
    mean = summed[:, :width] / summed[:, width : width + 1]
    means = to_all(jnp.broadcast_to(mean[None], (blocks, rows, width)), BLOCKS)

    at = lax.axis_index(RING).astype(jnp.int32).reshape(1)
    debiased = None
    for k in range(CHUNKS):
        totals = chip_sums(own[k], prev[k], own[0], prev[0], cols)
        same = to_all(totals, "y")
        swap = lax.ppermute(same, "core", [(0, 1), (1, 0)])
        debiased = debias(at, p, near, same, swap, own[0], prev[0], k, debiased)

    parts = jnp.sum(deviations(own, prev, means, cols), axis=(1, 2))
    mine = mean.reshape(rows, nodes, piece).swapaxes(0, 1)
    sent = jnp.concatenate(
        [mine, jnp.broadcast_to(parts[:, None, None], (nodes, rows, LANES - piece))], axis=2
    )
    sent = jnp.broadcast_to(sent[:, None], (nodes, splits, rows, LANES))
    got = to_all(sent.reshape(nodes * splits, rows, LANES), (*RING, "blk"))
    spread = jnp.sum(got[:, 0, piece : piece + 1], axis=0) / (rows_all * splits * hidden)
    got = got.reshape(nodes, splits, rows, LANES)
    average = lax.dynamic_index_in_dim(got, lax.axis_index("blk"), 1, keepdims=False)
    average = average[:, :, :piece].reshape(rows_all, piece)
    return debiased[None], average, spread


def solution(mesh):
    finer = Mesh(
        mesh.devices.reshape(2, 8, 4, 2, mesh.shape["blk"]),
        (*NODE, "blk"),
    )
    return jax.shard_map(
        body,
        mesh=finer,
        in_specs=(P(NODE, "blk", None), P(NODE)),
        out_specs=(P(NODE, "blk", None), P("blk", NODE), P(NODE)),
        check_vma=False,
    )
```

time: 189 us -> 201 us (1.063)
  waiting for transfers between devices: 77.5 us -> 99.8 us
  Pallas kernels: 32.2 us -> 24.7 us
  starting transfers between devices: 42.2 us -> 40 us
    all_to_all x7 -> x6, waiting for transfers between devices: 40.9 us -> 54.3 us  [to_all(): return lax.all_to_all(value, axes, 0, 0, tiled=True)]
    ppermute x3, waiting for transfers between devices: 36.7 us -> 45.5 us  [moved(): lax.ppermute(value, NODE, [(i, where(i) % node_count) for i in range(node...]
    pallas_call x2, Pallas kernels: 13.1 us -> 9.15 us  [debias(): pl.pallas_call(debias_body, grid_spec=pltpu.PrefetchScalarGridSpec(num_sc...]
    pallas_call x4 -> x3, Pallas kernels: 15.1 us -> 11.8 us  [the longest x2 7.42 us: chip_sums(): pl.pallas_call(chip_sums_body, grid=(steps,), in_specs=[pl.BlockSpec((nod...]
    all_to_all x7 -> x6, starting transfers between devices: 38.6 us -> 36.4 us  [to_all(): return lax.all_to_all(value, axes, 0, 0, tiled=True)]
  transfers between devices with their start and end apart: 12 -> 11, of which waited for: 7 -> 6; matrix products, arithmetic and copies ran while one was open for 3% -> 3% of each run, Pallas kernels for 12% -> 8%
where the time goes in v2:
time: 201 us; the launch traced here: 198 us
  waiting for transfers between devices  99.8 us (50%)
  starting transfers between devices  40 us (20%)
  Pallas kernels  24.7 us (12%)
  blocking collectives  19 us (9%)
  local copies, waits for them, and re-layouts  8.2 us (4%)
  between operations  3.24 us (2%)
  other arithmetic  2.86 us (1%)
    all_to_all x6, waiting for transfers between devices, to_all(): return lax.all_to_all(value, axes, 0, 0, tiled=True)  54.3 us
    ppermute x3, waiting for transfers between devices, moved(): lax.ppermute(value, NODE, [(i, where(i) % node_count) for i in range(node...  45.5 us
    all_to_all x6, starting transfers between devices, to_all(): return lax.all_to_all(value, axes, 0, 0, tiled=True)  36.4 us
    all_to_all x1, blocking collectives, to_all(): return lax.all_to_all(value, axes, 0, 0, tiled=True)  19 us
    pallas_call x2, Pallas kernels, debias(): pl.pallas_call(debias_body, grid_spec=pltpu.PrefetchScalarGridSpec(num_sc...  9.15 us
    pallas_call x2, Pallas kernels, chip_sums(): pl.pallas_call(chip_sums_body, grid=(steps,), in_specs=[pl.BlockSpec((nod...  7.42 us
    pallas_call x1, Pallas kernels, deviations(): pl.pallas_call(deviations_body, grid=(steps,), in_specs=[*[near(nodes, q)...  4.35 us
  transfers between devices with their start and end apart: 11, of which 6 were waited for; matrix products, arithmetic and copies ran while one was open for 3% of the time, Pallas kernels for 8%

profile of v2, /device:TPU:2, one launch (start us, length us, event | category | flops | bytes accessed | tf_op | source)
XLA Modules:
  0.0 197.9 jit_solution(6085914218039023287)
XLA Ops:
  0.7 2.3 %slice_bitcast_fusion = bf16[8,8,7168]{2,1,0:T(8,128)(2,1)} fusion(bf16[64,14336]{1,0:T(8,128)(2,1)} %bitcast.18), kind=kLoop, calls=%fused_computation.2 | loop fusion | bytes 1835008 | tf_op jit(solution)/shard_map/reshape | solution.py:247
  2.9 4.5 %all-to-all-start = ((bf16[8,8,7168]{2,1,0:T(8,128)(2,1)}), bf16[8,8,7168]{2,1,0:T(8,128)(2,1)S(1)}, u32[]{:S(2)}, u32[]{:S(2)}) async-start(bf16[8,8,7168]{2,1,0:T(8,128)(2,1)} %slice_bitcast_fusion), calls=%async_computation | async-start | bytes 1835008 | tf_op jit(solution)/shard_map/all_to_all | solution.py:18
  8.1 1.1 fusion
  9.2 12.8 %all-to-all-done.own_ref.b_ref.refs_1_ = bf16[8,8,7168]{2,1,0:T(8,128)(2,1)S(1)} async-done(((bf16[8,8,7168]{2,1,0:T(8,128)(2,1)}), bf16[8,8,7168]{2,1,0:T(8,128)(2,1)S(1)}, u32[]{:S(2)}, u32[]{:S(2)}) %all-to-all-start) | async-done | bytes 917536 | tf_op jit(solution)/shard_map/all_to_all | solution.py:18
  21.9 19.0 %all_to_all.35.w_ref.own_ref.a_ref.refs_0_.refs_4_ = bf16[8,8,7296]{2,1,0:T(8,128)(2,1)} all-to-all(bf16[8,8,7296]{2,1,0:T(8,128)(2,1)} %fusion), channel_id=1, replica_groups=mesh['xl'=2,'z'=8,'y'=4,'core'=2,'blk'=2] {'y','core'}, dimensions={0} | all-to-all | bytes 1867776 | tf_op jit(solution)/shard_map/all_to_all | solution.py:18
  40.9 3.8 %block_sums.1 = f32[16,8,1024]{2,1,0:T(8,128)} custom-call(bf16[8,8,7296]{2,1,0:T(8,128)(2,1)} %all_to_all.35.w_ref.own_ref.a_ref.refs_0_.refs_4_, bf16[8,8,7168]{2,1,0:T(8,128)(2,1)} %copy-done.2, bf16[8,8,7296]{2,1,0:T(8,128)(2,1)} %all_to_all.35.w_ref.own_ref.a_ref.refs_0_.refs_4_), custom_call_target="tpu_custom_call" | custom-call | tf_op jit(solution)/shard_map/block_sums/pallas_call | solution.py:55
  44.7 10.1 %all-to-all-start.4 = ((f32[16,8,1024]{2,1,0:T(8,128)}), f32[16,8,1024]{2,1,0:T(8,128)S(1)}, u32[]{:S(2)}, u32[]{:S(2)}) async-start(f32[16,8,1024]{2,1,0:T(8,128)} %block_sums.1), calls=%async_computation.4 | async-start | bytes 1048576 | tf_op jit(solution)/shard_map/all_to_all | solution.py:18
  54.9 1.5 collective-permute-start.2
  56.5 1.5 collective-permute-start.1
  58.0 45.5 %collective-permute-done.1.prev_ref.refs_3_ = bf16[7,8,7168]{2,1,0:T(8,128)(2,1)S(1)} collective-permute-done((bf16[7,8,7168]{2,1,0:T(8,128)(2,1)S(1)}, bf16[7,8,7168]{2,1,0:T(8,128)(2,1)S(1)}, u32[]{:S(2)}, u32[]{:S(2)}) %collective-permute-start.1) | collective-permute-done | bytes 802848 | tf_op jit(solution)/shard_map/ppermute | solution.py:240
  103.6 0.9 copy-done.7
  104.5 0.9 copy-done.1
  105.4 3.6 %chip_sums.2 = f32[4,8,7168]{2,1,0:T(8,128)} custom-call(bf16[8,8,7168]{2,1,0:T(8,128)(2,1)} %copy-done.2, bf16[7,8,7168]{2,1,0:T(8,128)(2,1)} %copy-done.7, bf16[8,8,7296]{2,1,0:T(8,128)(2,1)} %all_to_all.35.w_ref.own_ref.a_ref.refs_0_.refs_4_, bf16[7,8,7296]{2,1,0:T(8,128)(2,1)} %copy-done.1), custom_call_target="tpu_custom_call" | custom-call | tf_op jit(solution)/shard_map/chip_sums/pallas_call | solution.py:95
  109.1 0.8 copy-done.8
  109.9 3.5 %all-to-all-start.2 = ((f32[4,8,7168]{2,1,0:T(8,128)}), f32[4,8,7168]{2,1,0:T(8,128)S(1)}, u32[]{:S(2)}, u32[]{:S(2)}) async-start(f32[4,8,7168]{2,1,0:T(8,128)} %chip_sums.2), calls=%async_computation.2 | async-start | bytes 1835008 | tf_op jit(solution)/shard_map/all_to_all | solution.py:18
  113.4 3.8 %chip_sums.3 = f32[4,8,7168]{2,1,0:T(8,128)} custom-call(bf16[8,8,7296]{2,1,0:T(8,128)(2,1)} %all_to_all.35.w_ref.own_ref.a_ref.refs_0_.refs_4_, bf16[7,8,7296]{2,1,0:T(8,128)(2,1)} %copy-done.1, bf16[8,8,7296]{2,1,0:T(8,128)(2,1)} %all_to_all.35.w_ref.own_ref.a_ref.refs_0_.refs_4_, bf16[7,8,7296]{2,1,0:T(8,128)(2,1)} %copy-done.1), custom_call_target="tpu_custom_call" | custom-call | tf_op jit(solution)/shard_map/chip_sums/pallas_call | solution.py:95
  117.2 9.4 %all-to-all-done.2.same_ref = f32[4,8,7168]{2,1,0:T(8,128)S(1)} async-done(((f32[4,8,7168]{2,1,0:T(8,128)}), f32[4,8,7168]{2,1,0:T(8,128)S(1)}, u32[]{:S(2)}, u32[]{:S(2)}) %all-to-all-start.2) | async-done | bytes 917536 | tf_op jit(solution)/shard_map/all_to_all | solution.py:18
  126.6 4.2 %all-to-all-start.3 = ((f32[4,8,7168]{2,1,0:T(8,128)}), f32[4,8,7168]{2,1,0:T(8,128)}, u32[]{:S(2)}, u32[]{:S(2)}) async-start(f32[4,8,7168]{2,1,0:T(8,128)} %chip_sums.3), calls=%async_computation.3 | async-start | bytes 1835008 | tf_op jit(solution)/shard_map/all_to_all | solution.py:18
  131.2 12.1 %all-to-all-done.3.same_ref = f32[4,8,7168]{2,1,0:T(8,128)} async-done(((f32[4,8,7168]{2,1,0:T(8,128)}), f32[4,8,7168]{2,1,0:T(8,128)}, u32[]{:S(2)}, u32[]{:S(2)}) %all-to-all-start.3) | async-done | bytes 917536 | tf_op jit(solution)/shard_map/all_to_all | solution.py:18
  143.3 0.8 broadcast_in_dim.9
  144.1 6.9 %all-to-all-start.5 = ((f32[16,8,896]{2,1,0:T(8,128)}), f32[16,8,896]{2,1,0:T(8,128)S(1)}, u32[]{:S(2)}, u32[]{:S(2)}) async-start(f32[16,8,896]{2,1,0:T(8,128)} %broadcast_in_dim.9), calls=%async_computation.5 | async-start | bytes 917504 | tf_op jit(solution)/shard_map/all_to_all | solution.py:18
  151.6 12.2 %all-to-all-done.5.refs_6_ = f32[16,8,896]{2,1,0:T(8,128)S(1)} async-done(((f32[16,8,896]{2,1,0:T(8,128)}), f32[16,8,896]{2,1,0:T(8,128)S(1)}, u32[]{:S(2)}, u32[]{:S(2)}) %all-to-all-start.5) | async-done | bytes 458784 | tf_op jit(solution)/shard_map/all_to_all | solution.py:18
  163.8 0.8 copy-done.10
  164.6 4.3 %deviations.1 = f32[8,8,128]{2,1,0:T(8,128)} custom-call(bf16[8,8,7296]{2,1,0:T(8,128)(2,1)} %all_to_all.35.w_ref.own_ref.a_ref.refs_0_.refs_4_, bf16[8,8,7168]{2,1,0:T(8,128)(2,1)} %copy-done.2, bf16[7,8,7296]{2,1,0:T(8,128)(2,1)} %copy-done.1, bf16[7,8,7168]{2,1,0:T(8,128)(2,1)} %copy-done.7, ...), custom_call_target="tpu_custom_call" | custom-call | tf_op jit(solution)/shard_map/deviations/pallas_call | solution.py:162
  168.9 0.9 reduce_sum.28
  170.0 0.6 broadcast_in_dim.11
  170.6 7.2 %all-to-all-start.6 = ((f32[16,8,128]{2,1,0:T(8,128)}), f32[16,8,128]{2,1,0:T(8,128)S(1)}, u32[]{:S(2)}, u32[]{:S(2)}) async-start(f32[16,8,128]{2,1,0:T(8,128)} %bitcast.7), calls=%async_computation.6 | async-start | bytes 131072 | tf_op jit(solution)/shard_map/all_to_all | solution.py:18
  177.9 7.7 %all-to-all-done.6 = f32[16,8,128]{2,1,0:T(8,128)S(1)} async-done(((f32[16,8,128]{2,1,0:T(8,128)}), f32[16,8,128]{2,1,0:T(8,128)S(1)}, u32[]{:S(2)}, u32[]{:S(2)}) %all-to-all-start.6) | async-done | bytes 65568 | tf_op jit(solution)/shard_map/all_to_all | solution.py:18
  185.6 0.7 slice_reduce_fusion
  187.0 0.6 slice_bitcast_fusion.1
  187.6 4.6 %debias.2.rest_0_ = f32[64,14336]{1,0:T(8,128)} custom-call(s32[1]{0:T(128)} %bitcast.at_ref, bf16[64,14336]{1,0:T(8,128)(2,1)} %bitcast.19, bf16[64,14336]{1,0:T(8,128)(2,1)} %collective-permute-done.near_ref, f32[4,8,7168]{2,1,0:T(8,128)} %all-to-all-done.3.same_ref, f32[4,8,7168]{2,1,0:T(8,128)} %collective-permute-done.4.swap_ref, ...), custom_call_target="tpu_custom_call" | custom-call | tf_op jit(solution)/shard_map/debias/pallas_call | solution.py:213
  192.2 4.6 %debias.3 = f32[64,14336]{1,0:T(8,128)} custom-call(s32[1]{0:T(128)} %bitcast.at_ref, bf16[64,14336]{1,0:T(8,128)(2,1)} %bitcast.20, bf16[64,14336]{1,0:T(8,128)(2,1)} %collective-permute-done.near_ref, f32[4,8,7168]{2,1,0:T(8,128)} %copy-done.6, f32[4,8,7168]{2,1,0:T(8,128)} %collective-permute-done.3.swap_ref, ...), custom_call_target="tpu_custom_call", output_to_operand_aliasing={{}: (7, {})} | custom-call | tf_op jit(solution)/shard_map/debias/pallas_call | solution.py:213
  (38 shorter events, 1.2 us)
Async XLA Ops:
  0.6 7.4 %copy-start.4 = (bf16[1,64,14336]{2,1,0:T(8,128)(2,1)S(1)}, bf16[1,64,14336]{2,1,0:T(8,128)(2,1)}, u32[]{:S(2)}) copy-start(bf16[1,64,14336]{2,1,0:T(8,128)(2,1)} %param.2) | copy-start | bytes 5505028
  0.6 7.4 %copy-start.11 = (pred[7296]{0:T(1024)(128)(4,1)S(1)}, pred[7296]{0:T(1024)(128)(4,1)}, u32[]{:S(2)}) copy-start(pred[7296]{0:T(1024)(128)(4,1)} %constant.22.clone.1) | copy-start | bytes 21892
  2.9 19.0 %all-to-all-start = ((bf16[8,8,7168]{2,1,0:T(8,128)(2,1)}), bf16[8,8,7168]{2,1,0:T(8,128)(2,1)S(1)}, u32[]{:S(2)}, u32[]{:S(2)}) async-start(bf16[8,8,7168]{2,1,0:T(8,128)(2,1)} %slice_bitcast_fusion), calls=%async_computation | async-start | bytes 1835008 | tf_op jit(solution)/shard_map/all_to_all | solution.py:18
  21.9 19.0 %copy-start.2 = (bf16[8,8,7168]{2,1,0:T(8,128)(2,1)}, bf16[8,8,7168]{2,1,0:T(8,128)(2,1)S(1)}, u32[]{:S(2)}) copy-start(bf16[8,8,7168]{2,1,0:T(8,128)(2,1)S(1)} %all-to-all-done.own_ref.b_ref.refs_1_) | copy-start | bytes 2752516
  40.9 13.9 %copy-start = (bf16[8,8,7296]{2,1,0:T(8,128)(2,1)S(1)}, bf16[8,8,7296]{2,1,0:T(8,128)(2,1)}, u32[]{:S(2)}) copy-start(bf16[8,8,7296]{2,1,0:T(8,128)(2,1)} %all_to_all.35.w_ref.own_ref.a_ref.refs_0_.refs_4_) | copy-start | bytes 2801668
  44.7 11.7 %copy-start.3 = (bf16[8,8,7168]{2,1,0:T(8,128)(2,1)S(1)}, bf16[8,8,7168]{2,1,0:T(8,128)(2,1)}, u32[]{:S(2)}) copy-start(bf16[8,8,7168]{2,1,0:T(8,128)(2,1)} %copy-done.2) | copy-start | bytes 2752516
  44.7 64.3 %all-to-all-start.4 = ((f32[16,8,1024]{2,1,0:T(8,128)}), f32[16,8,1024]{2,1,0:T(8,128)S(1)}, u32[]{:S(2)}, u32[]{:S(2)}) async-start(f32[16,8,1024]{2,1,0:T(8,128)} %block_sums.1), calls=%async_computation.4 | async-start | bytes 1048576 | tf_op jit(solution)/shard_map/all_to_all | solution.py:18
  54.9 48.7 %collective-permute-start.2 = (bf16[7,8,7296]{2,1,0:T(8,128)(2,1)S(1)}, bf16[7,8,7296]{2,1,0:T(8,128)(2,1)S(1)}, u32[]{:S(2)}, u32[]{:S(2)}) collective-permute-start(bf16[7,8,7296]{2,1,0:T(8,128)(2,1)S(1)} %slice.36), channel_id=1, source_target_pairs={{0,16},{2,18},{4,20},{6,22},{8,24},{10,26},{12,28},{14,30},{16,32}... | collective-permute-start | bytes 2451464 | tf_op jit(solution)/shard_map/ppermute | solution.py:240
  56.5 47.1 %collective-permute-start.1 = (bf16[7,8,7168]{2,1,0:T(8,128)(2,1)S(1)}, bf16[7,8,7168]{2,1,0:T(8,128)(2,1)S(1)}, u32[]{:S(2)}, u32[]{:S(2)}) collective-permute-start(bf16[7,8,7168]{2,1,0:T(8,128)(2,1)S(1)} %slice.34), channel_id=1, source_target_pairs={{0,16},{2,18},{4,20},{6,22},{8,24},{10,26},{12,28},{14,30},{16,32}... | collective-permute-start | bytes 2408456 | tf_op jit(solution)/shard_map/ppermute | solution.py:240
  103.6 0.9 copy-start.7
  104.5 0.9 copy-start.1
  109.1 0.8 copy-start.8
  109.9 16.7 %all-to-all-start.2 = ((f32[4,8,7168]{2,1,0:T(8,128)}), f32[4,8,7168]{2,1,0:T(8,128)S(1)}, u32[]{:S(2)}, u32[]{:S(2)}) async-start(f32[4,8,7168]{2,1,0:T(8,128)} %chip_sums.2), calls=%async_computation.2 | async-start | bytes 1835008 | tf_op jit(solution)/shard_map/all_to_all | solution.py:18
  113.4 17.6 %copy-start.9 = (f32[16,8,1024]{2,1,0:T(8,128)S(1)}, f32[16,8,1024]{2,1,0:T(8,128)}, u32[]{:S(2)}) copy-start(f32[16,8,1024]{2,1,0:T(8,128)} %copy-done.8) | copy-start | bytes 1572868
  117.2 13.7 %copy-start.5 = (bf16[1,64,14336]{2,1,0:T(8,128)(2,1)S(1)}, bf16[1,64,14336]{2,1,0:T(8,128)(2,1)}, u32[]{:S(2)}) copy-start(bf16[1,64,14336]{2,1,0:T(8,128)(2,1)} %param.2) | copy-start | bytes 5505028
  126.6 24.4 %copy-start.6 = (f32[4,8,7168]{2,1,0:T(8,128)}, f32[4,8,7168]{2,1,0:T(8,128)S(1)}, u32[]{:S(2)}) copy-start(f32[4,8,7168]{2,1,0:T(8,128)S(1)} %all-to-all-done.2.same_ref) | copy-start | bytes 2752516
  126.6 16.7 %all-to-all-start.3 = ((f32[4,8,7168]{2,1,0:T(8,128)}), f32[4,8,7168]{2,1,0:T(8,128)}, u32[]{:S(2)}, u32[]{:S(2)}) async-start(f32[4,8,7168]{2,1,0:T(8,128)} %chip_sums.3), calls=%async_computation.3 | async-start | bytes 1835008 | tf_op jit(solution)/shard_map/all_to_all | solution.py:18
  130.9 56.7 %collective-permute-start = (bf16[64,14336]{1,0:T(8,128)(2,1)S(1)}, bf16[64,14336]{1,0:T(8,128)(2,1)}, u32[]{:S(2)}, u32[]{:S(2)}) collective-permute-start(bf16[64,14336]{1,0:T(8,128)(2,1)S(1)} %bitcast.22), channel_id=1, source_target_pairs={{0,2},{2,16},{4,6},{6,20},{8,10},{10,24},{12,14},{14,28},{16,18},{... | collective-permute-start | bytes 5505032 | tf_op jit(solution)/shard_map/ppermute | solution.py:240
  144.1 19.7 %all-to-all-start.5 = ((f32[16,8,896]{2,1,0:T(8,128)}), f32[16,8,896]{2,1,0:T(8,128)S(1)}, u32[]{:S(2)}, u32[]{:S(2)}) async-start(f32[16,8,896]{2,1,0:T(8,128)} %broadcast_in_dim.9), calls=%async_computation.5 | async-start | bytes 917504 | tf_op jit(solution)/shard_map/all_to_all | solution.py:18
  151.0 36.6 %collective-permute-start.4 = (f32[4,8,7168]{2,1,0:T(8,128)}, f32[4,8,7168]{2,1,0:T(8,128)}, u32[]{:S(2)}, u32[]{:S(2)}) collective-permute-start(f32[4,8,7168]{2,1,0:T(8,128)} %all-to-all-done.3.same_ref), channel_id=1, source_target_pairs={{0,2},{2,0},{1,3},{3,1},{4,6},{6,4},{5,7},{7,5},{8,10},{10,8},{9,1... | collective-permute-start | bytes 2752520 | tf_op jit(solution)/shard_map/ppermute | solution.py:259
  151.0 41.2 %collective-permute-start.3 = (f32[4,8,7168]{2,1,0:T(8,128)S(1)}, f32[4,8,7168]{2,1,0:T(8,128)}, u32[]{:S(2)}, u32[]{:S(2)}) collective-permute-start(f32[4,8,7168]{2,1,0:T(8,128)S(1)} %all-to-all-done.2.same_ref), channel_id=1, source_target_pairs={{0,2},{2,0},{1,3},{3,1},{4,6},{6,4},{5,7},{7,5},{8,10},{10,8},{9,1... | collective-permute-start | bytes 2752520 | tf_op jit(solution)/shard_map/ppermute | solution.py:259
  163.8 0.8 copy-start.10
  170.6 15.0 %all-to-all-start.6 = ((f32[16,8,128]{2,1,0:T(8,128)}), f32[16,8,128]{2,1,0:T(8,128)S(1)}, u32[]{:S(2)}, u32[]{:S(2)}) async-start(f32[16,8,128]{2,1,0:T(8,128)} %bitcast.7), calls=%async_computation.6 | async-start | bytes 131072 | tf_op jit(solution)/shard_map/all_to_all | solution.py:18

commit v3 on v2

v3 whole, which is shorter than its diff:
```python
import jax
import jax.numpy as jnp
from jax import lax
from jax.experimental import pallas as pl
from jax.experimental.pallas import tpu as pltpu
from jax.sharding import Mesh
from jax.sharding import PartitionSpec as P

NODE = ("xl", "z", "y", "core")
RING = ("y", "core")
BLOCKS = ("xl", "z")
CHUNKS = 2
LANES = 128
F32 = jnp.float32


def to_all(value, axes):
    return lax.all_to_all(value, axes, 0, 0, tiled=True)


def columns(ref):
    return [ref[k].astype(F32) for k in range(ref.shape[0])]


def block_sums_body(own_ref, w_ref, out_ref):
    pieces, _, wide = out_ref.shape
    width = wide - LANES
    w = columns(w_ref)
    total = sum(w[1:], w[0])
    for q in range(pieces):
        for t in range(width // LANES):
            at = slice(q * width + t * LANES, q * width + (t + 1) * LANES)
            acc = w[0] * own_ref[0, :, at].astype(F32)
            for k in range(1, len(w)):
                acc = acc + w[k] * own_ref[k, :, at].astype(F32)
            out_ref[q, :, t * LANES : (t + 1) * LANES] = acc
        out_ref[q, :, width:] = total


def whole(array):
    return pl.BlockSpec(array.shape, lambda *_: (0,) * array.ndim)


def block_sums(own, w, width, blocks):
    nodes, rows, _ = own.shape
    pieces = 4
    return pl.pallas_call(
        block_sums_body,
        grid=(blocks // pieces,),
        in_specs=[pl.BlockSpec((nodes, rows, pieces * width), lambda s: (0, 0, s)), whole(w)],
        out_specs=pl.BlockSpec((pieces, rows, width + LANES), lambda s: (s, 0, 0)),
        out_shape=jax.ShapeDtypeStruct((blocks, rows, width + LANES), F32),
        name="block_sums",
    )(own, w)


def chip_sums_body(at_ref, own_ref, prev_ref, w_ref, v_ref, *out_refs):
    w, v = columns(w_ref), columns(v_ref)
    chips = len(out_refs)
    width = out_refs[0].shape[1]
    here = at_ref[0] // 2
    for t in range(width // LANES):
        at = slice(t * LANES, (t + 1) * LANES)
        after = [None] * chips
        for y in range(chips - 1, 0, -1):
            k = 2 * y
            pair = v[k] * prev_ref[k - 1, :, at].astype(F32)
            pair = pair + v[k + 1] * prev_ref[k, :, at].astype(F32)
            after[y - 1] = pair if after[y] is None else after[y] + pair
        before, sums = None, []
        for y in range(chips):
            parts = [part for part in (before, after[y]) if part is not None]
            sums.append(sum(parts[1:], parts[0]))
            if y < chips - 1:
                k = 2 * y
                pair = w[k] * own_ref[k, :, at].astype(F32)
                pair = pair + w[k + 1] * own_ref[k + 1, :, at].astype(F32)
                before = pair if before is None else before + pair
        for k in range(chips):
            chosen = sums[k]
            for y in range(1, chips):
                chosen = jnp.where(here == y, sums[y ^ k], chosen)
            out_refs[k][:, at] = chosen


def chip_sums(at, own, prev, w, v, chunk):
    nodes, rows = own.shape[:2]
    cols = prev.shape[2]
    steps = 4
    width = cols // steps
    chips = nodes // 2
    return pl.pallas_call(
        chip_sums_body,
        grid_spec=pltpu.PrefetchScalarGridSpec(
            num_scalar_prefetch=1,
            grid=(steps,),
            in_specs=[
                pl.BlockSpec((nodes, rows, width), lambda s, at: (0, 0, chunk * steps + s)),
                pl.BlockSpec((nodes - 1, rows, width), lambda s, at: (0, 0, s)),
                whole(w),
                whole(v),
            ],
            out_specs=[pl.BlockSpec((rows, width), lambda s, at: (0, s))] * chips,
        ),
        out_shape=[jax.ShapeDtypeStruct((rows, cols), F32)] * chips,
        name="chip_sums",
    )(at, own, prev, w, v)


def deviations_body(*refs):
    own_ref, prev_refs = refs[0], refs[1 : 1 + CHUNKS]
    w_ref, v_ref, means_ref, out_ref = refs[1 + CHUNKS :]
    w, v = columns(w_ref), columns(v_ref)
    nodes = len(w)
    pieces, _, width = means_ref.shape
    inverse = []
    for c in range(nodes):
        terms = w[: c + 1] + v[c + 1 :]
        inverse.append(1.0 / sum(terms[1:], terms[0]))
    step = pl.program_id(0)

    @pl.when(step == 0)
    def _():
        out_ref[...] = jnp.zeros(out_ref.shape, F32)

    def fill(prev_ref):
        accs = [out_ref[c] for c in range(nodes)]
        for q in range(pieces):
            for t in range(width // LANES):
                at = slice(q * width + t * LANES, q * width + (t + 1) * LANES)
                mean = means_ref[q, :, t * LANES : (t + 1) * LANES]
                after = [None] * nodes
                for c in range(nodes - 1, 0, -1):
                    term = v[c] * prev_ref[c - 1, :, at].astype(F32)
                    after[c - 1] = term if after[c] is None else after[c] + term
                before = None
                for c in range(nodes):
                    term = w[c] * own_ref[c, :, at].astype(F32)
                    before = term if before is None else before + term
                    value = before if after[c] is None else before + after[c]
                    gap = value * inverse[c] - mean
                    accs[c] = accs[c] + gap * gap
        for c in range(nodes):
            out_ref[c] = accs[c]

    per = pl.num_programs(0) // CHUNKS
    for q in range(CHUNKS):
        pl.when(step // per == q)(lambda q=q: fill(prev_refs[q]))


def deviations(own, prev, w, v, means):
    nodes, rows, _ = own.shape
    blocks, _, piece = means.shape
    pieces = 4
    steps = blocks // pieces
    per = steps // CHUNKS
    width = pieces * piece

    def near(q):
        return pl.BlockSpec(
            (nodes - 1, rows, width), lambda s: (0, 0, jnp.clip(s - q * per, 0, per - 1))
        )

    return pl.pallas_call(
        deviations_body,
        grid=(steps,),
        in_specs=[
            pl.BlockSpec((nodes, rows, width), lambda s: (0, 0, s)),
            *[near(q) for q in range(CHUNKS)],
            whole(w),
            whole(v),
            pl.BlockSpec((pieces, rows, piece), lambda s: (s, 0, 0)),
        ],
        out_specs=pl.BlockSpec((nodes, rows, LANES), lambda s: (0, 0, 0)),
        out_shape=jax.ShapeDtypeStruct((nodes, rows, LANES), F32),
        name="deviations",
    )(own, *prev, w, v, means)


def debias_body(at_ref, p_ref, near_ref, *refs):
    chips = (len(refs) - 3) // 2
    same_refs, swap_refs = refs[:chips], refs[chips : 2 * chips]
    w_ref, v_ref = refs[2 * chips : 2 * chips + 2]
    out_ref = refs[-1]
    c = at_ref[0]
    even = c % 2 == 0
    rows = w_ref.shape[1]
    w, v = ([value[:, 0:1] for value in columns(ref)] for ref in (w_ref, v_ref))
    scale = own = other = w[0]
    for k in range(1, len(w)):
        scale = scale + jnp.where(k <= c, w[k], v[k])
        own = jnp.where(k == c, w[k], own)
        if k % 2:
            other = jnp.where(k == c + 1, v[k], other)
        else:
            other = jnp.where(k == c - 1, w[k], other)
    inverse = 1.0 / scale
    own, other = own * inverse, other * inverse
    for k in range(chips):
        at = pl.ds(pl.multiple_of(2 * rows * ((c // 2) ^ k), 2 * rows), 2 * rows)
        same, swap = same_refs[k][...] * inverse, swap_refs[k][...] * inverse
        halves = (jnp.where(even, same, swap), jnp.where(even, swap, same))
        p, near = p_ref[at].astype(F32), near_ref[at].astype(F32)
        parts = [
            total + own * p[h * rows : (h + 1) * rows] + other * near[h * rows : (h + 1) * rows]
            for h, total in enumerate(halves)
        ]
        out_ref[at] = jnp.concatenate(parts, axis=0)


def debias(at, p, near, same, swap, w, v, chunk, so_far):
    rows, cols = same[0].shape
    steps = 4
    width = cols // steps
    wide = pl.BlockSpec((p.shape[0], width), lambda s, at: (0, chunk * steps + s))
    part = pl.BlockSpec((rows, width), lambda s, at: (0, s))
    in_specs = [wide, wide, *[part] * (len(same) + len(swap)), whole(w), whole(v)]
    operands = [at, p, near, *same, *swap, w, v]
    body = debias_body
    aliases = {}
    if so_far is not None:
        in_specs.append(pl.BlockSpec(memory_space=pl.ANY))
        operands.append(so_far)
        aliases = {len(operands) - 1: 0}
        body = lambda *refs: debias_body(*refs[:-2], refs[-1])
    return pl.pallas_call(
        body,
        grid_spec=pltpu.PrefetchScalarGridSpec(
            num_scalar_prefetch=1,
            grid=(steps,),
            in_specs=in_specs,
            out_specs=wide,
        ),
        out_shape=jax.ShapeDtypeStruct(p.shape, F32),
        input_output_aliases=aliases,
        name="debias",
    )(*operands)


def body(params, weights):
    p = params[0]
    node_count = lax.axis_size(NODE)
    nodes = lax.axis_size(RING)
    blocks = lax.axis_size(BLOCKS)
    splits = lax.axis_size("blk")
    rows_all, hidden = p.shape
    rows = rows_all // nodes
    cols = hidden // CHUNKS
    width = hidden // blocks
    piece = width // nodes

    def moved(value, where):
        return lax.ppermute(value, NODE, [(i, where(i) % node_count) for i in range(node_count)])

    near = moved(p, lambda i: i + 1 if i % 2 == 0 else i + nodes - 1)
    own = to_all(p.reshape(nodes, rows, hidden), RING)
    at = lax.axis_index(RING).astype(jnp.int32)
    place = jnp.arange(nodes)[:, None, None] == at
    w = jnp.where(place, weights.astype(F32)[0], 0.0)
    w = jnp.broadcast_to(w, (nodes, rows, LANES))
    for step in (1, 2, 4):
        w = w + moved(w, lambda i, step=step: i ^ step)
    v = moved(w, lambda i: i + nodes)
    at = at.reshape(1)
    prev = []
    for k in range(CHUNKS):
        prev.append(moved(own[1:, :, k * cols : (k + 1) * cols], lambda i: i + nodes))

    summed = jnp.sum(to_all(block_sums(own, w, width, blocks), BLOCKS), axis=0)
    mean = summed[:, :width] / summed[:, width : width + 1]
    means = to_all(jnp.broadcast_to(mean[None], (blocks, rows, width)), BLOCKS)

    debiased = None
    for k in range(CHUNKS):
        same = list(chip_sums(at, own, prev[k], w, v, k))
        for step in range(1, len(same)):
            same[step] = moved(same[step], lambda i, step=step: i ^ (2 * step))
        swap = [moved(value, lambda i: i ^ 1) for value in same]
        debiased = debias(at, p, near, same, swap, w, v, k, debiased)

    parts = jnp.sum(deviations(own, prev, w, v, means), axis=(1, 2))
    mine = mean.reshape(rows, nodes, piece).swapaxes(0, 1)
    sent = jnp.concatenate(
        [mine, jnp.broadcast_to(parts[:, None, None], (nodes, rows, LANES - piece))], axis=2
    )
    sent = jnp.broadcast_to(sent[:, None], (nodes, splits, rows, LANES))
    got = to_all(sent.reshape(nodes * splits, rows, LANES), (*RING, "blk"))
    spread = jnp.sum(got[:, 0, piece : piece + 1], axis=0) / (rows_all * splits * hidden)
    got = got.reshape(nodes, splits, rows, LANES)
    average = lax.dynamic_index_in_dim(got, lax.axis_index("blk"), 1, keepdims=False)
    average = average[:, :, :piece].reshape(rows_all, piece)
    return debiased[None], average, spread


def solution(mesh):
    finer = Mesh(
        mesh.devices.reshape(2, 8, 4, 2, mesh.shape["blk"]),
        (*NODE, "blk"),
    )
    return jax.shard_map(
        body,
        mesh=finer,
        in_specs=(P(NODE, "blk", None), P(NODE)),
        out_specs=(P(NODE, "blk", None), P("blk", NODE), P(NODE)),
        check_vma=False,
    )
```

time: 201 us -> 170 us (0.85)
  the two profiles are of different devices: /device:TPU:2 before, /device:TPU:1 now
where the time goes in v3:
time: 170 us; the launch traced here: 169 us
  waiting for transfers between devices  85.5 us (50%)
  starting transfers between devices  43.9 us (26%)
  Pallas kernels  24 us (14%)
  local copies, waits for them, and re-layouts  9.38 us (6%)
  between operations  3.32 us (2%)
  other arithmetic  2.54 us (1%)
    ppermute x21, waiting for transfers between devices, moved(): lax.ppermute(value, NODE, [(i, where(i) % node_count) for i in range(node...  61.3 us
    all_to_all x4, starting transfers between devices, to_all(): return lax.all_to_all(value, axes, 0, 0, tiled=True)  24.7 us
    all_to_all x4, waiting for transfers between devices, to_all(): return lax.all_to_all(value, axes, 0, 0, tiled=True)  24.2 us
    ppermute x21, starting transfers between devices, moved(): lax.ppermute(value, NODE, [(i, where(i) % node_count) for i in range(node...  19.2 us
    pallas_call x2, Pallas kernels, debias(): pl.pallas_call(body, grid_spec=pltpu.PrefetchScalarGridSpec(num_scalar_pr...  8.85 us
    pallas_call x2, Pallas kernels, chip_sums(): pl.pallas_call(chip_sums_body, grid_spec=pltpu.PrefetchScalarGridSpec(num...  7.42 us
    unnamed x36, local copies, waits for them, and re-layouts  4.57 us
    pallas_call x1, Pallas kernels, deviations(): pl.pallas_call(deviations_body, grid=(steps,), in_specs=[pl.BlockSpec((no...  4.23 us
  transfers between devices with their start and end apart: 25, of which 8 were waited for; matrix products, arithmetic and copies ran while one was open for 4% of the time, Pallas kernels for 14%

profile of v3, /device:TPU:1, one launch (start us, length us, event | category | flops | bytes accessed | tf_op | source)
XLA Modules:
  0.0 168.7 jit_solution(14767926211462011751)
XLA Ops:
  0.6 6.7 %all-to-all-start = ((bf16[8,8,14336]{2,1,0:T(8,128)(2,1)}), bf16[8,8,14336]{2,1,0:T(8,128)(2,1)S(1)}, u32[]{:S(2)}, u32[]{:S(2)}) async-start(bf16[8,8,14336]{2,1,0:T(8,128)(2,1)} %bitcast.15), calls=%async_computation | async-start | bytes 3670016 | tf_op jit(solution)/shard_map/all_to_all | solution.py:18
  8.2 1.1 collective-permute-done.2
  9.4 1.4 collective-permute-start.3
  10.8 19.1 %collective-permute-done.3 = f32[8,8,128]{2,1,0:T(8,128)S(1)} collective-permute-done((f32[8,8,128]{2,1,0:T(8,128)S(1)}, f32[8,8,128]{2,1,0:T(8,128)S(1)}, u32[]{:S(2)}, u32[]{:S(2)}) %collective-permute-start.3) | collective-permute-done | bytes 32800 | tf_op jit(solution)/shard_map/ppermute | solution.py:253
  30.0 2.2 %collective-permute-start.4 = (f32[8,8,128]{2,1,0:T(8,128)S(1)}, f32[8,8,128]{2,1,0:T(8,128)S(1)}, u32[]{:S(2)}, u32[]{:S(2)}) collective-permute-start(f32[8,8,128]{2,1,0:T(8,128)S(1)} %fusion.1), channel_id=1, source_target_pairs={{0,8},{2,10},{4,12},{6,14},{8,0},{10,2},{12,4},{14,6},{16,24},{18,... | collective-permute-start | bytes 98312 | tf_op jit(solution)/shard_map/ppermute | solution.py:253
  32.2 2.3 %collective-permute-start = (bf16[64,14336]{1,0:T(8,128)(2,1)}, bf16[64,14336]{1,0:T(8,128)(2,1)}, u32[]{:S(2)}, u32[]{:S(2)}) collective-permute-start(bf16[64,14336]{1,0:T(8,128)(2,1)} %bitcast.16), channel_id=1, source_target_pairs={{0,2},{2,16},{4,6},{6,20},{8,10},{10,24},{12,14},{14,28},{16,18},{... | collective-permute-start | bytes 5505032 | tf_op jit(solution)/shard_map/ppermute | solution.py:253
  35.1 1.2 copy-done
  36.3 3.5 %block_sums.1 = f32[16,8,1024]{2,1,0:T(8,128)} custom-call(bf16[8,8,14336]{2,1,0:T(8,128)(2,1)} %copy-done, f32[8,8,128]{2,1,0:T(8,128)} %add.19.w_ref.refs_8_.refs_11_.refs_3_), custom_call_target="tpu_custom_call" | custom-call | tf_op jit(solution)/shard_map/block_sums/pallas_call | solution.py:47
  39.9 8.3 %all-to-all-start.1 = ((f32[16,8,1024]{2,1,0:T(8,128)}), f32[16,8,1024]{2,1,0:T(8,128)S(1)}, u32[]{:S(2)}, u32[]{:S(2)}) async-start(f32[16,8,1024]{2,1,0:T(8,128)} %block_sums.1), calls=%async_computation.1 | async-start | bytes 1048576 | tf_op jit(solution)/shard_map/all_to_all | solution.py:18
  48.2 2.4 %fusion = (bf16[7,8,7168]{2,1,0:T(8,128)(2,1)}, bf16[7,8,7168]{2,1,0:T(8,128)(2,1)S(1)}) fusion(bf16[8,8,14336]{2,1,0:T(8,128)(2,1)} %copy-done), kind=kLoop, calls=%fused_computation.9 | loop fusion | bytes 3211264 | tf_op jit(solution)/shard_map/slice | solution.py:267
  50.6 1.4 collective-permute-start.13
  51.9 1.2 collective-permute-start.1
  53.1 24.2 %all-to-all-done.1 = f32[16,8,1024]{2,1,0:T(8,128)S(1)} async-done(((f32[16,8,1024]{2,1,0:T(8,128)}), f32[16,8,1024]{2,1,0:T(8,128)S(1)}, u32[]{:S(2)}, u32[]{:S(2)}) %all-to-all-start.1) | async-done | bytes 524320 | tf_op jit(solution)/shard_map/all_to_all | solution.py:18
  77.6 0.8 broadcast_in_dim.39
  78.4 5.0 %all-to-all-start.2 = ((f32[16,8,896]{2,1,0:T(8,128)}), f32[16,8,896]{2,1,0:T(8,128)S(1)}, u32[]{:S(2)}, u32[]{:S(2)}) async-start(f32[16,8,896]{2,1,0:T(8,128)} %broadcast_in_dim.39), calls=%async_computation.2 | async-start | bytes 917504 | tf_op jit(solution)/shard_map/all_to_all | solution.py:18
  83.3 1.4 collective-permute-start.5
  84.8 31.1 %collective-permute-done.5.v_ref.refs_9_.refs_12_.refs_4_ = f32[8,8,128]{2,1,0:T(8,128)S(1)} collective-permute-done((f32[8,8,128]{2,1,0:T(8,128)S(1)}, f32[8,8,128]{2,1,0:T(8,128)S(1)}, u32[]{:S(2)}, u32[]{:S(2)}) %collective-permute-start.5) | collective-permute-done | bytes 32800 | tf_op jit(solution)/shard_map/ppermute | solution.py:253
  116.8 3.7 %chip_sums.3 = (f32[8,7168]{1,0:T(8,128)}, f32[8,7168]{1,0:T(8,128)}, f32[8,7168]{1,0:T(8,128)}, f32[8,7168]{1,0:T(8,128)}) custom-call(s32[1]{0:T(128)} %bitcast.at_ref.refs_0_, bf16[8,8,14336]{2,1,0:T(8,128)(2,1)} %copy-done, bf16[7,8,7168]{2,1,0:T(8,128)(2,1)} %copy-done.1, f32[8,8,128]{2,1,0:T(8,128)} %add.19.w_ref.refs_8_.refs_11_.refs_3_, ...), custom_call_target="tpu_custom_call" | custom-call | tf_op jit(solution)/shard_map/chip_sums/pallas_call | solution.py:92
  120.5 1.1 collective-permute-start.14
  121.6 2.1 %collective-permute-start.15 = (f32[8,7168]{1,0:T(8,128)}, f32[8,7168]{1,0:T(8,128)S(1)}, u32[]{:S(2)}, u32[]{:S(2)}) collective-permute-start(f32[8,7168]{1,0:T(8,128)} %get-tuple-element.17), channel_id=1, source_target_pairs={{0,8},{2,10},{4,12},{6,14},{8,0},{10,2},{12,4},{14,6},{16,24},{18,... | collective-permute-start | bytes 688136 | tf_op jit(solution)/shard_map/ppermute | solution.py:253
  124.4 0.9 copy-done.2
  125.3 3.7 %chip_sums.2 = (f32[8,7168]{1,0:T(8,128)}, f32[8,7168]{1,0:T(8,128)}, f32[8,7168]{1,0:T(8,128)}, f32[8,7168]{1,0:T(8,128)}) custom-call(s32[1]{0:T(128)} %bitcast.at_ref.refs_0_, bf16[8,8,14336]{2,1,0:T(8,128)(2,1)} %copy-done, bf16[7,8,7168]{2,1,0:T(8,128)(2,1)} %copy-done.2, f32[8,8,128]{2,1,0:T(8,128)} %add.19.w_ref.refs_8_.refs_11_.refs_3_, ...), custom_call_target="tpu_custom_call" | custom-call | tf_op jit(solution)/shard_map/chip_sums/pallas_call | solution.py:92
  129.1 3.2 %collective-permute-start.7 = (f32[8,7168]{1,0:T(8,128)}, f32[8,7168]{1,0:T(8,128)S(1)}, u32[]{:S(2)}, u32[]{:S(2)}) collective-permute-start(f32[8,7168]{1,0:T(8,128)} %get-tuple-element.13), channel_id=1, source_target_pairs={{0,8},{2,10},{4,12},{6,14},{8,0},{10,2},{12,4},{14,6},{16,24},{18,... | collective-permute-start | bytes 688136 | tf_op jit(solution)/shard_map/ppermute | solution.py:253
  133.5 3.4 %collective-permute-done.6.refs_4_ = f32[8,7168]{1,0:T(8,128)S(1)} collective-permute-done((f32[8,7168]{1,0:T(8,128)}, f32[8,7168]{1,0:T(8,128)S(1)}, u32[]{:S(2)}, u32[]{:S(2)}) %collective-permute-start.6) | collective-permute-done | bytes 229408 | tf_op jit(solution)/shard_map/ppermute | solution.py:253
  136.9 3.9 %collective-permute-done.7.refs_5_ = f32[8,7168]{1,0:T(8,128)S(1)} collective-permute-done((f32[8,7168]{1,0:T(8,128)}, f32[8,7168]{1,0:T(8,128)S(1)}, u32[]{:S(2)}, u32[]{:S(2)}) %collective-permute-start.7) | collective-permute-done | bytes 229408 | tf_op jit(solution)/shard_map/ppermute | solution.py:253
  140.8 2.5 %collective-permute-done.8.refs_6_ = f32[8,7168]{1,0:T(8,128)S(1)} collective-permute-done((f32[8,7168]{1,0:T(8,128)}, f32[8,7168]{1,0:T(8,128)S(1)}, u32[]{:S(2)}, u32[]{:S(2)}) %collective-permute-start.8) | collective-permute-done | bytes 229408 | tf_op jit(solution)/shard_map/ppermute | solution.py:253
  144.4 0.8 copy-done.3
  145.2 4.2 %deviations.1 = f32[8,8,128]{2,1,0:T(8,128)} custom-call(bf16[8,8,14336]{2,1,0:T(8,128)(2,1)} %copy-done, bf16[7,8,7168]{2,1,0:T(8,128)(2,1)} %copy-done.1, bf16[7,8,7168]{2,1,0:T(8,128)(2,1)} %copy-done.2, f32[8,8,128]{2,1,0:T(8,128)} %add.19.w_ref.refs_8_.refs_11_.refs_3_, f32[8,8,128]{2,1,0:T(8,128)} %copy-done.5, f32[16,8,896]{2,1,0:T(8,128)} %copy-done.3), custom_call_target="tpu_custom_call" | custom-call | tf_op jit(solution)/shard_map/deviations/pallas_call | solution.py:164
  149.4 0.9 reduce_sum.28
  151.1 4.8 %all-to-all-start.3 = ((f32[16,8,128]{2,1,0:T(8,128)}), f32[16,8,128]{2,1,0:T(8,128)S(1)}, u32[]{:S(2)}, u32[]{:S(2)}) async-start(f32[16,8,128]{2,1,0:T(8,128)} %bitcast.6), calls=%async_computation.3 | async-start | bytes 131072 | tf_op jit(solution)/shard_map/all_to_all | solution.py:18
  155.9 4.4 %debias.2.refs_13_ = f32[64,14336]{1,0:T(8,128)} custom-call(s32[1]{0:T(128)} %bitcast.at_ref.refs_0_, bf16[64,14336]{1,0:T(8,128)(2,1)} %bitcast.17, bf16[64,14336]{1,0:T(8,128)(2,1)} %collective-permute-done.near_ref.refs_2_, f32[8,7168]{1,0:T(8,128)} %get-tuple-element.15.refs_0_, f32[8,7168]{1,0:T(8,128)} %copy-done.8, f32[8,7168]{1,0:T(8,128)} %copy-done.10, ...), custom_call_target="tpu_custom_call" | custom-call | tf_op jit(solution)/shard_map/debias/pallas_call | solution.py:226
  161.1 4.4 %debias.3 = f32[64,14336]{1,0:T(8,128)} custom-call(s32[1]{0:T(128)} %bitcast.at_ref.refs_0_, bf16[64,14336]{1,0:T(8,128)(2,1)} %bitcast.18, bf16[64,14336]{1,0:T(8,128)(2,1)} %collective-permute-done.near_ref.refs_2_, f32[8,7168]{1,0:T(8,128)} %get-tuple-element.11.refs_3_, f32[8,7168]{1,0:T(8,128)} %copy-done.6, ...), custom_call_target="tpu_custom_call", output_to_operand_aliasing={{}: (13, {})} | custom-call | tf_op jit(solution)/shard_map/debias/pallas_call | solution.py:226
  (79 shorter events, 8.1 us)
Async XLA Ops:
  0.6 34.5 %all-to-all-start = ((bf16[8,8,14336]{2,1,0:T(8,128)(2,1)}), bf16[8,8,14336]{2,1,0:T(8,128)(2,1)S(1)}, u32[]{:S(2)}, u32[]{:S(2)}) async-start(bf16[8,8,14336]{2,1,0:T(8,128)(2,1)} %bitcast.15), calls=%async_computation | async-start | bytes 3670016 | tf_op jit(solution)/shard_map/all_to_all | solution.py:18
  8.1 1.2 collective-permute-start.2
  9.4 20.6 %collective-permute-start.3 = (f32[8,8,128]{2,1,0:T(8,128)S(1)}, f32[8,8,128]{2,1,0:T(8,128)S(1)}, u32[]{:S(2)}, u32[]{:S(2)}) collective-permute-start(f32[8,8,128]{2,1,0:T(8,128)S(1)} %broadcast_add_fusion), channel_id=1, source_target_pairs={{0,4},{2,6},{4,0},{6,2},{8,12},{10,14},{12,8},{14,10},{16,20},{18,... | collective-permute-start | bytes 98312 | tf_op jit(solution)/shard_map/ppermute | solution.py:253
  30.0 4.4 %collective-permute-start.4 = (f32[8,8,128]{2,1,0:T(8,128)S(1)}, f32[8,8,128]{2,1,0:T(8,128)S(1)}, u32[]{:S(2)}, u32[]{:S(2)}) collective-permute-start(f32[8,8,128]{2,1,0:T(8,128)S(1)} %fusion.1), channel_id=1, source_target_pairs={{0,8},{2,10},{4,12},{6,14},{8,0},{10,2},{12,4},{14,6},{16,24},{18,... | collective-permute-start | bytes 98312 | tf_op jit(solution)/shard_map/ppermute | solution.py:253
  32.2 96.9 %collective-permute-start = (bf16[64,14336]{1,0:T(8,128)(2,1)}, bf16[64,14336]{1,0:T(8,128)(2,1)}, u32[]{:S(2)}, u32[]{:S(2)}) collective-permute-start(bf16[64,14336]{1,0:T(8,128)(2,1)} %bitcast.16), channel_id=1, source_target_pairs={{0,2},{2,16},{4,6},{6,20},{8,10},{10,24},{12,14},{14,28},{16,18},{... | collective-permute-start | bytes 5505032 | tf_op jit(solution)/shard_map/ppermute | solution.py:253
  39.9 37.5 %all-to-all-start.1 = ((f32[16,8,1024]{2,1,0:T(8,128)}), f32[16,8,1024]{2,1,0:T(8,128)S(1)}, u32[]{:S(2)}, u32[]{:S(2)}) async-start(f32[16,8,1024]{2,1,0:T(8,128)} %block_sums.1), calls=%async_computation.1 | async-start | bytes 1048576 | tf_op jit(solution)/shard_map/all_to_all | solution.py:18
  48.2 35.2 %copy-start.4 = (f32[8,8,128]{2,1,0:T(8,128)S(1)}, f32[8,8,128]{2,1,0:T(8,128)}, u32[]{:S(2)}) copy-start(f32[8,8,128]{2,1,0:T(8,128)} %add.19.w_ref.refs_8_.refs_11_.refs_3_) | copy-start | bytes 98308
  50.6 65.3 %collective-permute-start.13 = (bf16[7,8,7168]{2,1,0:T(8,128)(2,1)}, bf16[7,8,7168]{2,1,0:T(8,128)(2,1)S(1)}, u32[]{:S(2)}, u32[]{:S(2)}) collective-permute-start(bf16[7,8,7168]{2,1,0:T(8,128)(2,1)} %get-tuple-element.19), channel_id=1, source_target_pairs={{0,16},{2,18},{4,20},{6,22},{8,24},{10,26},{12,28},{14,30},{16,32}... | collective-permute-start | bytes 2408456 | tf_op jit(solution)/shard_map/ppermute | solution.py:253
  51.9 72.5 %collective-permute-start.1 = (bf16[7,8,7168]{2,1,0:T(8,128)(2,1)S(1)}, bf16[7,8,7168]{2,1,0:T(8,128)(2,1)S(1)}, u32[]{:S(2)}, u32[]{:S(2)}) collective-permute-start(bf16[7,8,7168]{2,1,0:T(8,128)(2,1)S(1)} %get-tuple-element.20), channel_id=1, source_target_pairs={{0,16},{2,18},{4,20},{6,22},{8,24},{10,26},{12,28},{14,30},{16,32}... | collective-permute-start | bytes 2408456 | tf_op jit(solution)/shard_map/ppermute | solution.py:253
  78.4 66.0 %all-to-all-start.2 = ((f32[16,8,896]{2,1,0:T(8,128)}), f32[16,8,896]{2,1,0:T(8,128)S(1)}, u32[]{:S(2)}, u32[]{:S(2)}) async-start(f32[16,8,896]{2,1,0:T(8,128)} %broadcast_in_dim.39), calls=%async_computation.2 | async-start | bytes 917504 | tf_op jit(solution)/shard_map/all_to_all | solution.py:18
  83.3 32.5 %collective-permute-start.5 = (f32[8,8,128]{2,1,0:T(8,128)S(1)}, f32[8,8,128]{2,1,0:T(8,128)S(1)}, u32[]{:S(2)}, u32[]{:S(2)}) collective-permute-start(f32[8,8,128]{2,1,0:T(8,128)S(1)} %copy-done.4), channel_id=1, source_target_pairs={{0,16},{2,18},{4,20},{6,22},{8,24},{10,26},{12,28},{14,30},{16,32}... | collective-permute-start | bytes 98312 | tf_op jit(solution)/shard_map/ppermute | solution.py:253
  120.5 11.8 %collective-permute-start.14 = (f32[8,7168]{1,0:T(8,128)}, f32[8,7168]{1,0:T(8,128)S(1)}, u32[]{:S(2)}, u32[]{:S(2)}) collective-permute-start(f32[8,7168]{1,0:T(8,128)} %get-tuple-element.16), channel_id=1, source_target_pairs={{0,4},{2,6},{4,0},{6,2},{8,12},{10,14},{12,8},{14,10},{16,20},{18,... | collective-permute-start | bytes 688136 | tf_op jit(solution)/shard_map/ppermute | solution.py:253
  121.6 11.3 %collective-permute-start.15 = (f32[8,7168]{1,0:T(8,128)}, f32[8,7168]{1,0:T(8,128)S(1)}, u32[]{:S(2)}, u32[]{:S(2)}) collective-permute-start(f32[8,7168]{1,0:T(8,128)} %get-tuple-element.17), channel_id=1, source_target_pairs={{0,8},{2,10},{4,12},{6,14},{8,0},{10,2},{12,4},{14,6},{16,24},{18,... | collective-permute-start | bytes 688136 | tf_op jit(solution)/shard_map/ppermute | solution.py:253
  123.8 9.5 %collective-permute-start.16 = (f32[8,7168]{1,0:T(8,128)}, f32[8,7168]{1,0:T(8,128)S(1)}, u32[]{:S(2)}, u32[]{:S(2)}) collective-permute-start(f32[8,7168]{1,0:T(8,128)} %get-tuple-element.18), channel_id=1, source_target_pairs={{0,12},{2,14},{4,8},{6,10},{8,4},{10,6},{12,0},{14,2},{16,28},{18,... | collective-permute-start | bytes 688136 | tf_op jit(solution)/shard_map/ppermute | solution.py:253
  129.0 7.9 %collective-permute-start.6 = (f32[8,7168]{1,0:T(8,128)}, f32[8,7168]{1,0:T(8,128)S(1)}, u32[]{:S(2)}, u32[]{:S(2)}) collective-permute-start(f32[8,7168]{1,0:T(8,128)} %get-tuple-element.12), channel_id=1, source_target_pairs={{0,4},{2,6},{4,0},{6,2},{8,12},{10,14},{12,8},{14,10},{16,20},{18,... | collective-permute-start | bytes 688136 | tf_op jit(solution)/shard_map/ppermute | solution.py:253
  129.1 11.7 %collective-permute-start.7 = (f32[8,7168]{1,0:T(8,128)}, f32[8,7168]{1,0:T(8,128)S(1)}, u32[]{:S(2)}, u32[]{:S(2)}) collective-permute-start(f32[8,7168]{1,0:T(8,128)} %get-tuple-element.13), channel_id=1, source_target_pairs={{0,8},{2,10},{4,12},{6,14},{8,0},{10,2},{12,4},{14,6},{16,24},{18,... | collective-permute-start | bytes 688136 | tf_op jit(solution)/shard_map/ppermute | solution.py:253
  132.3 23.6 %copy-start.8 = (f32[8,7168]{1,0:T(8,128)}, f32[8,7168]{1,0:T(8,128)S(1)}, u32[]{:S(2)}) copy-start(f32[8,7168]{1,0:T(8,128)S(1)} %collective-permute-done.14.refs_1_) | copy-start | bytes 688132
  132.3 11.0 %collective-permute-start.8 = (f32[8,7168]{1,0:T(8,128)}, f32[8,7168]{1,0:T(8,128)S(1)}, u32[]{:S(2)}, u32[]{:S(2)}) collective-permute-start(f32[8,7168]{1,0:T(8,128)} %get-tuple-element.14), channel_id=1, source_target_pairs={{0,12},{2,14},{4,8},{6,10},{8,4},{10,6},{12,0},{14,2},{16,28},{18,... | collective-permute-start | bytes 688136 | tf_op jit(solution)/shard_map/ppermute | solution.py:253
  132.9 22.9 %copy-start.10 = (f32[8,7168]{1,0:T(8,128)}, f32[8,7168]{1,0:T(8,128)S(1)}, u32[]{:S(2)}) copy-start(f32[8,7168]{1,0:T(8,128)S(1)} %collective-permute-done.15.refs_2_) | copy-start | bytes 688132
  132.9 10.3 %collective-permute-start.17 = (f32[8,7168]{1,0:T(8,128)S(1)}, f32[8,7168]{1,0:T(8,128)S(1)}, u32[]{:S(2)}, u32[]{:S(2)}) collective-permute-start(f32[8,7168]{1,0:T(8,128)S(1)} %copy-done.7), channel_id=1, source_target_pairs={{0,2},{2,0},{4,6},{6,4},{8,10},{10,8},{12,14},{14,12},{16,18},{18,... | collective-permute-start | bytes 688136 | tf_op jit(solution)/shard_map/ppermute | solution.py:253
  133.3 22.6 %copy-start.11 = (f32[8,7168]{1,0:T(8,128)}, f32[8,7168]{1,0:T(8,128)S(1)}, u32[]{:S(2)}) copy-start(f32[8,7168]{1,0:T(8,128)S(1)} %collective-permute-done.16.refs_3_) | copy-start | bytes 688132
  133.3 10.5 %collective-permute-start.18 = (f32[8,7168]{1,0:T(8,128)S(1)}, f32[8,7168]{1,0:T(8,128)S(1)}, u32[]{:S(2)}, u32[]{:S(2)}) collective-permute-start(f32[8,7168]{1,0:T(8,128)S(1)} %collective-permute-done.14.refs_1_), channel_id=1, source_target_pairs={{0,2},{2,0},{4,6},{6,4},{8,10},{10,8},{12,14},{14,12},{16,18},{18,... | collective-permute-start | bytes 688136 | tf_op jit(solution)/shard_map/ppermute | solution.py:253
  136.9 23.4 %copy-start.6 = (f32[8,7168]{1,0:T(8,128)}, f32[8,7168]{1,0:T(8,128)S(1)}, u32[]{:S(2)}) copy-start(f32[8,7168]{1,0:T(8,128)S(1)} %collective-permute-done.6.refs_4_) | copy-start | bytes 688132
  136.9 7.0 %collective-permute-start.19 = (f32[8,7168]{1,0:T(8,128)S(1)}, f32[8,7168]{1,0:T(8,128)S(1)}, u32[]{:S(2)}, u32[]{:S(2)}) collective-permute-start(f32[8,7168]{1,0:T(8,128)S(1)} %collective-permute-done.15.refs_2_), channel_id=1, source_target_pairs={{0,2},{2,0},{4,6},{6,4},{8,10},{10,8},{12,14},{14,12},{16,18},{18,... | collective-permute-start | bytes 688136 | tf_op jit(solution)/shard_map/ppermute | solution.py:253
  140.8 19.6 %copy-start.9 = (f32[8,7168]{1,0:T(8,128)}, f32[8,7168]{1,0:T(8,128)S(1)}, u32[]{:S(2)}) copy-start(f32[8,7168]{1,0:T(8,128)S(1)} %collective-permute-done.7.refs_5_) | copy-start | bytes 688132
  140.8 19.6 %collective-permute-start.9 = (f32[8,7168]{1,0:T(8,128)}, f32[8,7168]{1,0:T(8,128)S(1)}, u32[]{:S(2)}, u32[]{:S(2)}) collective-permute-start(f32[8,7168]{1,0:T(8,128)} %get-tuple-element.11.refs_3_), channel_id=1, source_target_pairs={{0,2},{2,0},{4,6},{6,4},{8,10},{10,8},{12,14},{14,12},{16,18},{18,... | collective-permute-start | bytes 688136 | tf_op jit(solution)/shard_map/ppermute | solution.py:253
  143.2 17.1 %copy-start.12 = (f32[8,7168]{1,0:T(8,128)}, f32[8,7168]{1,0:T(8,128)S(1)}, u32[]{:S(2)}) copy-start(f32[8,7168]{1,0:T(8,128)S(1)} %collective-permute-done.8.refs_6_) | copy-start | bytes 688132
  143.3 12.6 %collective-permute-start.20 = (f32[8,7168]{1,0:T(8,128)S(1)}, f32[8,7168]{1,0:T(8,128)}, u32[]{:S(2)}, u32[]{:S(2)}) collective-permute-start(f32[8,7168]{1,0:T(8,128)S(1)} %collective-permute-done.16.refs_3_), channel_id=1, source_target_pairs={{0,2},{2,0},{4,6},{6,4},{8,10},{10,8},{12,14},{14,12},{16,18},{18,... | collective-permute-start | bytes 688136 | tf_op jit(solution)/shard_map/ppermute | solution.py:253
  143.3 17.1 %collective-permute-start.10 = (f32[8,7168]{1,0:T(8,128)S(1)}, f32[8,7168]{1,0:T(8,128)S(1)}, u32[]{:S(2)}, u32[]{:S(2)}) collective-permute-start(f32[8,7168]{1,0:T(8,128)S(1)} %collective-permute-done.6.refs_4_), channel_id=1, source_target_pairs={{0,2},{2,0},{4,6},{6,4},{8,10},{10,8},{12,14},{14,12},{16,18},{18,... | collective-permute-start | bytes 688136 | tf_op jit(solution)/shard_map/ppermute | solution.py:253
  143.8 16.6 %collective-permute-start.11 = (f32[8,7168]{1,0:T(8,128)S(1)}, f32[8,7168]{1,0:T(8,128)}, u32[]{:S(2)}, u32[]{:S(2)}) collective-permute-start(f32[8,7168]{1,0:T(8,128)S(1)} %collective-permute-done.7.refs_5_), channel_id=1, source_target_pairs={{0,2},{2,0},{4,6},{6,4},{8,10},{10,8},{12,14},{14,12},{16,18},{18,... | collective-permute-start | bytes 688136 | tf_op jit(solution)/shard_map/ppermute | solution.py:253
  143.9 16.5 %collective-permute-start.12 = (f32[8,7168]{1,0:T(8,128)S(1)}, f32[8,7168]{1,0:T(8,128)}, u32[]{:S(2)}, u32[]{:S(2)}) collective-permute-start(f32[8,7168]{1,0:T(8,128)S(1)} %collective-permute-done.8.refs_6_), channel_id=1, source_target_pairs={{0,2},{2,0},{4,6},{6,4},{8,10},{10,8},{12,14},{14,12},{16,18},{18,... | collective-permute-start | bytes 688136 | tf_op jit(solution)/shard_map/ppermute | solution.py:253
  151.1 14.5 %all-to-all-start.3 = ((f32[16,8,128]{2,1,0:T(8,128)}), f32[16,8,128]{2,1,0:T(8,128)S(1)}, u32[]{:S(2)}, u32[]{:S(2)}) async-start(f32[16,8,128]{2,1,0:T(8,128)} %bitcast.6), calls=%async_computation.3 | async-start | bytes 131072 | tf_op jit(solution)/shard_map/all_to_all | solution.py:18
  (11 other events, 55.1 us)
